TPU v7x, 16 devices: a 4x2x1 block of a 4x4x8 slice. The times are simulated.
16 devices in a mesh: rep: 4 (over y, z, core), dp: 4 (over x).
Axes of the slice: x: 4, y: 2, z: 1, core: 2. Of those that a mesh axis runs over, the one named last changes fastest.
The devices are a block of a 4x4x8 slice.
Arguments:
- x: bfloat16 [16, 4096, 768], P(('rep', 'dp')), parts along dimension 0
- dy: bfloat16 [16, 4096, 768], P(('rep', 'dp')), parts along dimension 0
- w_gate: bfloat16 [2, 768, 1792], P(None, 'dp')
- w_up: bfloat16 [2, 768, 1792], P(None, 'dp')
- w_down: bfloat16 [2, 1792, 768], P(None, 'dp')
Outputs:
- output 1: bfloat16 [16, 4096, 768], P(('rep', 'dp')), parts along dimension 0
- output 2: bfloat16 [8, 768, 1792], P('rep', 'dp'), parts along dimension 0
- output 3: bfloat16 [8, 768, 1792], P('rep', 'dp'), parts along dimension 0
- output 4: bfloat16 [8, 1792, 768], P('rep', 'dp'), parts along dimension 0
There are 4 independent parts. A program takes and returns all parts, laid end to end along the dimension named above; an argument that names none is the same for every part.
All inputs are finite; a program needn't handle non-finite values.
Results may differ from a plain program's by a relative error of at most 0.018.
Values are sent between devices in bfloat16 or wider.
A program may use at most 768 MiB of HBM per device.

v0:
```python
import jax
import jax.numpy as jnp
from jax import lax

NAMES = ("w_gate", "w_up", "w_down")


def matmul(a, w):
    return jnp.dot(a, w, preferred_element_type=jnp.float32).astype(jnp.bfloat16)


def normed(h):
    wide = h.astype(jnp.float32)
    scale = lax.rsqrt(jnp.mean(wide**2, -1, keepdims=True) + 1e-6)
    return (wide * scale).astype(jnp.bfloat16)


def layer(h, w):
    a = normed(h)
    gate = jnp.dot(a, w["w_gate"], preferred_element_type=jnp.float32)
    up = jnp.dot(a, w["w_up"], preferred_element_type=jnp.float32)
    return h + matmul((jax.nn.silu(gate) * up).astype(jnp.bfloat16), w["w_down"])


def stack(weights, h):
    for number in range(weights["w_gate"].shape[0]):
        h = layer(h, {name: w[number] for name, w in weights.items()})
    return h


def solution(mesh):
    groups = mesh.shape["rep"]

    def step(x, dy, *weights):
        shape = x.shape
        x, dy = (t.reshape(groups, -1, *t.shape[1:]) for t in (x, dy))

        def of_a_group(x, dy):
            _, back = jax.vjp(stack, dict(zip(NAMES, weights, strict=True)), x)
            by_weights, by_x = back(dy)
            return (by_x, *(by_weights[name] for name in NAMES))

        by_x, *by_weights = jax.vmap(of_a_group)(x, dy)
        return (by_x.reshape(shape), *(t.reshape(-1, *t.shape[2:]) for t in by_weights))

    return step
```

profile of v0, /device:TPU:112, one launch (start us, length us, event | category | flops | bytes accessed | tf_op | source)
XLA Modules:
  0.0 673.9 jit_solution(13123295847106026894)
XLA Ops:
  44.7 19.8 %fusion.111 = f32[4096,1792]{1,0:T(8,128)} fusion(bf16[1,768,1792]{2,1,0:T(8,128)(2,1)} %all-gather.30.cloned.1.call-done, bf16[1,4096,768]{2,1,0:T(8,128)(2,1)} %param.1, f32[4096]{0:T(1024)S(1)} %get-tuple-element.13), kind=kOutput, calls=%fused_computation.105 | convolution fusion | flops 11283726336 | bytes 38420480 | tf_op jit(solution)/vmap(jvp())/dot_general | solution.py:20
  64.4 14.4 %all-gather.32.cloned.1.call-done = bf16[1,768,1792]{2,1,0:T(8,128)(2,1)} async-done(((bf16[1,192,1792]{2,1,0:T(8,128)(2,1)}), bf16[1,768,1792]{2,1,0:T(8,128)(2,1)}) %all-gather.32.cloned.1.call-update) | async-done | bytes 2752528 | tf_op jit(solution)/vmap(jvp())/squeeze | solution.py:27
  78.9 19.8 %fusion.108 = f32[4096,1792]{1,0:T(8,128)} fusion(bf16[1,768,1792]{2,1,0:T(8,128)(2,1)} %all-gather.32.cloned.1.call-done, bf16[1,4096,768]{2,1,0:T(8,128)(2,1)} %param.1, f32[4096]{0:T(1024)S(1)} %get-tuple-element.13), kind=kOutput, calls=%fused_computation.102 | convolution fusion | flops 11283726336 | bytes 38420480 | tf_op jit(solution)/vmap(jvp())/dot_general | solution.py:21
  98.6 25.9 %fusion.24 = bf16[4096,1792]{1,0:T(8,128)(2,1)} fusion(f32[4096,1792]{1,0:T(8,128)} %fusion.108, f32[4096,1792]{1,0:T(8,128)} %fusion.111), kind=kLoop, calls=%fused_computation.47 | loop fusion | flops 44040192 | bytes 73400320
  124.6 19.4 %fusion.40 = (f32[4096]{0:T(1024)S(1)}, bf16[1,1,4096,768]{2,3,1,0:T(8,128)(2,1)}) fusion(bf16[4096,1792]{1,0:T(8,128)(2,1)} %fusion.24, bf16[1,1792,768]{2,1,0:T(8,128)(2,1)} %all-gather.34.cloned.1.call-done, bf16[1,4096,768]{1,2,0:T(8,128)(2,1)} %copy.1), kind=kOutput, calls=%fused_computation.62 | convolution fusion | flops 11290013696 | bytes 30031872 | tf_op jit(solution)/vmap(jvp())/dot_general | solution.py:9
  146.6 19.8 %fusion.74 = f32[4096,1792]{1,0:T(8,128)} fusion(bf16[1,1,4096,768]{2,3,1,0:T(8,128)(2,1)} %get-tuple-element.15, f32[4096]{0:T(1024)S(1)} %bitcast.305, bf16[1,768,1792]{2,1,0:T(8,128)(2,1)} %all-gather.36.cloned.1.call-done), kind=kOutput, calls=%fused_computation.87 | convolution fusion | flops 11283726336 | bytes 38420480 | tf_op jit(solution)/vmap(jvp())/dot_general | solution.py:20
  166.4 14.2 %all-gather.40.cloned.1.call-done = bf16[1,768,1792]{2,1,0:T(8,128)(2,1)} async-done(((bf16[1,192,1792]{2,1,0:T(8,128)(2,1)}), bf16[1,768,1792]{2,1,0:T(8,128)(2,1)}) %all-gather.40.cloned.1.call-update) | async-done | bytes 2752528 | tf_op jit(solution)/vmap(jvp())/squeeze | solution.py:27
  180.6 19.9 %fusion.72 = f32[4096,1792]{1,0:T(8,128)} fusion(bf16[1,1,4096,768]{2,3,1,0:T(8,128)(2,1)} %get-tuple-element.15, f32[4096]{0:T(1024)S(1)} %bitcast.306, bf16[1,768,1792]{2,1,0:T(8,128)(2,1)} %all-gather.40.cloned.1.call-done), kind=kOutput, calls=%fused_computation.86 | convolution fusion | flops 11283726336 | bytes 38420480 | tf_op jit(solution)/vmap(jvp())/dot_general | solution.py:21
  200.5 13.6 %all-gather.38.cloned.1.call-done = bf16[1,1792,768]{2,1,0:T(8,128)(2,1)} async-done(((bf16[1,448,768]{2,1,0:T(8,128)(2,1)}), bf16[1,1792,768]{2,1,0:T(8,128)(2,1)}) %all-gather.38.cloned.1.call-update) | async-done | bytes 2752528 | tf_op jit(solution)/vmap(jvp())/squeeze | solution.py:27
  214.1 17.5 %convolution_convert_fusion.1 = bf16[4096,1792]{1,0:T(8,128)(2,1)} fusion(bf16[1,4096,768]{2,1,0:T(8,128)(2,1)} %param, bf16[1,1792,768]{2,1,0:T(8,128)(2,1)} %all-gather.38.cloned.1.call-done), kind=kOutput, calls=%fused_computation.46 | convolution fusion | flops 11281629184 | bytes 23724032 | tf_op jit(solution)/vmap(transpose(jvp()))/dot_general | solution.py:9
  231.6 24.6 %fusion.4 = bf16[4096,1792]{1,0:T(8,128)(2,1)S(1)} fusion(f32[4096,1792]{1,0:T(8,128)} %fusion.74, f32[4096,1792]{1,0:T(8,128)} %fusion.72, bf16[4096,1792]{1,0:T(8,128)(2,1)} %convolution_convert_fusion.1), kind=kLoop, calls=%fused_computation.10 | loop fusion | flops 88080384 | bytes 88080384
  274.7 25.1 %fusion.42 = (f32[4096]{0:T(1024)S(1)}, bf16[4096,768]{0,1:T(8,128)(2,1)}) fusion(bf16[1,1,4096,768]{2,3,1,0:T(8,128)(2,1)} %get-tuple-element.15, bf16[4096,768]{0,1:T(8,128)(2,1)} %convolution_convert_fusion.3, bf16[1,768,1792]{2,1,0:T(8,128)(2,1)S(1)} %copy-done.11, bf16[4096,1792]{1,0:T(8,128)(2,1)} %convolution_convert_fusion.1, f32[4096,1792]{1,0:T(8,128)} %fusion.74), kind=kOutput, calls=%fused_computation.64 | convolution fusion | flops 11337199616 | bytes 65683456 | tf_op jit(solution)/vmap(transpose(jvp()))/dot_general | solution.py:21
  310.9 17.0 %fusion.91 = f32[1,1792,768]{2,1,0:T(8,128)} fusion(bf16[4096,1792]{1,0:T(8,128)(2,1)} %fusion.24, bf16[1,1,4096,768]{2,3,1,0:T(8,128)(2,1)S(1)} %fusion.53), kind=kOutput, calls=%fused_computation.91 | convolution fusion | flops 11274289152 | bytes 26476544 | tf_op jit(solution)/vmap(transpose(jvp()))/dot_general | solution.py:9
  328.0 26.6 %fusion.76 = f32[1,1792,768]{2,1,0:T(8,128)} fusion(bf16[1,4096,768]{2,1,0:T(8,128)(2,1)} %param, f32[4096,1792]{1,0:T(8,128)} %fusion.72, f32[4096,1792]{1,0:T(8,128)} %fusion.74), kind=kOutput, calls=%fused_computation.88 | convolution fusion | flops 11318329344 | bytes 70516736 | tf_op jit(solution)/vmap(transpose(jvp()))/dot_general | solution.py:9
  354.8 19.7 %convolution_convert_fusion = bf16[4096,1792]{1,0:T(8,128)(2,1)} fusion(bf16[1,1,4096,768]{2,3,1,0:T(8,128)(2,1)} %copy-done, bf16[1,1792,768]{2,1,0:T(8,128)(2,1)S(1)} %copy-done.9), kind=kOutput, calls=%fused_computation.45 | convolution fusion | flops 11281629184 | bytes 23724032 | tf_op jit(solution)/vmap(transpose(jvp()))/dot_general | solution.py:9
  374.5 30.1 %fusion.7 = bf16[4096,1792]{1,0:T(8,128)(2,1)} fusion(f32[4096,1792]{1,0:T(8,128)} %fusion.111, f32[4096,1792]{1,0:T(8,128)} %fusion.108, bf16[4096,1792]{1,0:T(8,128)(2,1)} %convolution_convert_fusion), kind=kLoop, calls=%fused_computation.13 | loop fusion | flops 88080384 | bytes 88080384
  404.6 25.4 %fusion.81 = f32[1,768,1792]{2,1,0:T(8,128)} fusion(bf16[4096,1792]{1,0:T(8,128)(2,1)} %convolution_convert_fusion.1, f32[4096,1792]{1,0:T(8,128)} %fusion.74, bf16[1,1,4096,768]{2,3,1,0:T(8,128)(2,1)} %get-tuple-element.15, f32[4096]{0:T(1024)S(1)} %bitcast.308), kind=kOutput, calls=%fused_computation.89 | convolution fusion | flops 11327766528 | bytes 55853056 | tf_op jit(solution)/vmap(transpose(jvp()))/dot_general | solution.py:21
  430.2 16.8 %convolution_convert_fusion.2 = bf16[4096,768]{0,1:T(8,128)(2,1)} fusion(bf16[4096,1792]{1,0:T(8,128)(2,1)} %fusion.7, bf16[1,768,1792]{2,1,0:T(8,128)(2,1)S(1)} %copy-done.8), kind=kOutput, calls=%fused_computation.67 | convolution fusion | flops 11274289152 | bytes 23724032 | tf_op jit(solution)/vmap(transpose(jvp()))/dot_general | solution.py:20
  447.0 26.0 %fusion.38 = (f32[4096]{0:T(1024)S(1)}, bf16[4096,768]{0,1:T(8,128)(2,1)}) fusion(bf16[1,4096,768]{1,2,0:T(8,128)(2,1)} %copy.1, bf16[4096,768]{0,1:T(8,128)(2,1)} %convolution_convert_fusion.2, bf16[1,768,1792]{2,1,0:T(8,128)(2,1)} %all-gather.32.cloned.1.call-done, bf16[4096,1792]{1,0:T(8,128)(2,1)} %convolution_convert_fusion, f32[4096,1792]{1,0:T(8,128)} %fusion.111), kind=kOutput, calls=%fused_computation.60 | convolution fusion | flops 11337199616 | bytes 65683456 | tf_op jit(solution)/vmap(transpose(jvp()))/dot_general | solution.py:21
  473.7 25.8 %fusion.86 = f32[1,768,1792]{2,1,0:T(8,128)} fusion(bf16[4096,1792]{1,0:T(8,128)(2,1)} %convolution_convert_fusion, f32[4096,1792]{1,0:T(8,128)} %fusion.111, bf16[1,4096,768]{1,2,0:T(8,128)(2,1)} %copy.1, f32[4096]{0:T(1024)S(1)} %bitcast.310), kind=kOutput, calls=%fused_computation.90 | convolution fusion | flops 11327766528 | bytes 55853056 | tf_op jit(solution)/vmap(transpose(jvp()))/dot_general | solution.py:21
  499.6 18.2 %fusion.94 = f32[1,768,1792]{2,1,0:T(8,128)} fusion(bf16[4096,1792]{1,0:T(8,128)(2,1)} %copy-done.1, bf16[1,1,4096,768]{2,3,1,0:T(8,128)(2,1)} %get-tuple-element.15, f32[4096]{0:T(1024)S(1)} %bitcast.309), kind=kOutput, calls=%fused_computation.92 | convolution fusion | flops 11283726336 | bytes 26492928 | tf_op jit(solution)/vmap(transpose(jvp()))/dot_general | solution.py:20
  517.9 18.3 %fusion.97 = f32[1,768,1792]{2,1,0:T(8,128)} fusion(bf16[4096,1792]{1,0:T(8,128)(2,1)} %fusion.7, bf16[1,4096,768]{1,2,0:T(8,128)(2,1)} %copy.1, f32[4096]{0:T(1024)S(1)} %bitcast.311), kind=kOutput, calls=%fused_computation.93 | convolution fusion | flops 11283726336 | bytes 26492928 | tf_op jit(solution)/vmap(transpose(jvp()))/dot_general | solution.py:20
  564.0 44.9 %reduce-scatter.19.cloned.1.call-done = f32[1,192,1792]{2,1,0:T(8,128)} async-done(((f32[1,768,1792]{2,1,0:T(8,128)}), f32[1,192,1792]{2,1,0:T(8,128)}) %reduce-scatter.19.cloned.1.call-update) | async-done | bytes 1376272
  610.3 53.9 %reduce-scatter.21.cloned.1.call-done = f32[1,192,1792]{2,1,0:T(8,128)} async-done(((f32[1,768,1792]{2,1,0:T(8,128)}), f32[1,192,1792]{2,1,0:T(8,128)}) %reduce-scatter.21.cloned.1.call-update) | async-done | bytes 1376272
  (79 shorter events, 102.5 us)
Async XLA Ops:
  7.2 37.5 %all-gather.30.cloned.1.call-start = ((), (), s32[]{:S(2)}) async-start(), calls=%async_computation.6 | async-start | bytes 3440640 | tf_op jit(solution)/vmap(jvp())/squeeze | solution.py:27
  9.8 69.1 %all-gather.32.cloned.1.call-start = ((), (), s32[]{:S(2)}) async-start(), calls=%async_computation.7 | async-start | bytes 3440640 | tf_op jit(solution)/vmap(jvp())/squeeze | solution.py:27
  12.4 112.2 %all-gather.34.cloned.1.call-start = ((), (), s32[]{:S(2)}) async-start(), calls=%async_computation.8 | async-start | bytes 3440640 | tf_op jit(solution)/vmap(jvp())/squeeze | solution.py:27
  15.0 131.5 %all-gather.36.cloned.1.call-start = ((), (), s32[]{:S(2)}) async-start(), calls=%async_computation.9 | async-start | bytes 3440640 | tf_op jit(solution)/vmap(jvp())/squeeze | solution.py:27
  15.7 164.9 %all-gather.40.cloned.1.call-start = ((), (), s32[]{:S(2)}) async-start(), calls=%async_computation.11 | async-start | bytes 3440640 | tf_op jit(solution)/vmap(jvp())/squeeze | solution.py:27
  16.3 197.8 %all-gather.38.cloned.1.call-start = ((), (), s32[]{:S(2)}) async-start(), calls=%async_computation.10 | async-start | bytes 3440640 | tf_op jit(solution)/vmap(jvp())/squeeze | solution.py:27
  16.9 539.0 %reduce-scatter.29.cloned.1.call-start = ((), (), s32[]{:S(2)}) async-start(), calls=%async_computation.17 | async-start | bytes 6881280
  144.0 0.6 copy-start.2
  144.6 260.0 %copy-start.4 = (f32[1,1,4096]{2,1,0:T(1,128)}, f32[1,1,4096]{2,1,0:T(1,128)S(1)}, u32[]{:S(2)}) copy-start(f32[1,1,4096]{2,1,0:T(1,128)S(1)} %rsqrt.23) | copy-start | bytes 49156
  231.6 29.8 %copy-start.10 = (bf16[1,768,1792]{2,1,0:T(8,128)(2,1)S(1)}, bf16[1,768,1792]{2,1,0:T(8,128)(2,1)}, u32[]{:S(2)}) copy-start(bf16[1,768,1792]{2,1,0:T(8,128)(2,1)} %all-gather.36.cloned.1.call-done) | copy-start | bytes 8257540
  256.2 5.2 copy-start.1
  261.4 13.3 %copy-start.11 = (bf16[1,768,1792]{2,1,0:T(8,128)(2,1)S(1)}, bf16[1,768,1792]{2,1,0:T(8,128)(2,1)}, u32[]{:S(2)}) copy-start(bf16[1,768,1792]{2,1,0:T(8,128)(2,1)} %all-gather.40.cloned.1.call-done) | copy-start | bytes 8257540
  274.7 25.1 %copy-start.3 = (f32[4096]{0:T(1024)S(1)}, f32[4096]{0:T(1024)}, u32[]{:S(2)}) copy-start(f32[4096]{0:T(1024)} %copy-done.2) | copy-start | bytes 49156
  308.3 2.6 copy-start
  328.0 26.9 %copy-start.9 = (bf16[1,1792,768]{2,1,0:T(8,128)(2,1)S(1)}, bf16[1,1792,768]{2,1,0:T(8,128)(2,1)}, u32[]{:S(2)}) copy-start(bf16[1,1792,768]{2,1,0:T(8,128)(2,1)} %all-gather.34.cloned.1.call-done) | copy-start | bytes 8257540
  328.0 229.5 %reduce-scatter.27.cloned.1.call-start = ((), (), s32[]{:S(2)}) async-start(), calls=%async_computation.16 | async-start | bytes 6881280
  354.7 205.3 %reduce-scatter.23.cloned.1.call-start = ((), (), s32[]{:S(2)}) async-start(), calls=%async_computation.14 | async-start | bytes 6881280
  404.6 25.6 %copy-start.8 = (bf16[1,768,1792]{2,1,0:T(8,128)(2,1)S(1)}, bf16[1,768,1792]{2,1,0:T(8,128)(2,1)}, u32[]{:S(2)}) copy-start(bf16[1,768,1792]{2,1,0:T(8,128)(2,1)} %all-gather.30.cloned.1.call-done) | copy-start | bytes 8257540
  430.1 131.3 %reduce-scatter.25.cloned.1.call-start = ((), (), s32[]{:S(2)}) async-start(), calls=%async_computation.15 | async-start | bytes 6881280
  447.0 26.0 %copy-start.7 = (f32[4096]{0:T(1024)S(1)}, f32[4096]{0:T(1024)}, u32[]{:S(2)}) copy-start(f32[4096]{0:T(1024)} %get-tuple-element.12) | copy-start | bytes 49156
  473.7 25.9 %copy-start.5 = (f32[1,1,4096]{2,1,0:T(1,128)S(1)}, f32[1,1,4096]{2,1,0:T(1,128)}, u32[]{:S(2)}) copy-start(f32[1,1,4096]{2,1,0:T(1,128)} %copy-done.4) | copy-start | bytes 49156
  499.5 109.4 %reduce-scatter.19.cloned.1.call-start = ((), (), s32[]{:S(2)}) async-start(), calls=%async_computation.12 | async-start | bytes 6881280
  517.8 18.4 %copy-start.6 = (f32[1,1,4096]{2,1,0:T(1,128)S(1)}, f32[1,1,4096]{2,1,0:T(1,128)}, u32[]{:S(2)}) copy-start(f32[1,1,4096]{2,1,0:T(1,128)} %get-tuple-element.11) | copy-start | bytes 49156
  517.8 146.5 %reduce-scatter.21.cloned.1.call-start = ((), (), s32[]{:S(2)}) async-start(), calls=%async_computation.13 | async-start | bytes 6881280
Sparse Core Ops, SparseCore 0:
  9.9 34.6 all-gather.29
  46.8 32.0 all-gather.31
  80.4 32.0 all-gather.33
  114.5 32.0 all-gather.35
  148.5 32.0 all-gather.39
  182.0 32.0 all-gather.37
  328.1 53.7 reduce-scatter.28
  384.2 53.1 reduce-scatter.26
  439.7 53.1 reduce-scatter.22
  499.6 53.7 reduce-scatter.24
  555.7 53.1 reduce-scatter.18
  611.1 53.1 reduce-scatter.20
where the time goes:
time: 677 us; the launch traced here: 674 us
  matrix products  348 us (51%)
  waiting for transfers between devices  151 us (22%)
  other arithmetic  117 us (17%)
  local copies, waits for them, and re-layouts  42.1 us (6%)
  between operations  14.6 us (2%)
    dot_general x6, matrix products, layer(): up = jnp.dot(a, w['w_up'], preferred_element_type=jnp.float32)  142 us
    dot_general x6, matrix products, layer(): gate = jnp.dot(a, w['w_gate'], preferred_element_type=jnp.float32)  106 us
    unnamed x18, waiting for transfers between devices  101 us
    dot_general x5, matrix products, matmul(): jnp.dot(a, w, preferred_element_type=jnp.float32).astype(jnp.bfloat16)  100 us
    unnamed x3, other arithmetic  80.6 us
    squeeze x6, waiting for transfers between devices, stack(): h = layer(h, {name: w[number] for name, w in weights.items()})  49.5 us
    unnamed x27, local copies, waits for them, and re-layouts  34.7 us
  transfers between devices with their start and end apart: 12, of which 7 were waited for; matrix products, arithmetic and copies ran while one was open for 58% of the time, Pallas kernels for 0%

commit v1 on v0

v1 whole, which is shorter than its diff:
```python
import functools

import jax
import jax.numpy as jnp
from jax import lax
from jax.experimental import pallas as pl
from jax.experimental.pallas import tpu as pltpu
from jax.sharding import PartitionSpec as P

F32, BF16 = jnp.float32, jnp.bfloat16
NT = (((1,), (1,)), ((), ()))
TN = (((0,), (0,)), ((), ()))
VMEM_LIMIT = 60 * 2**20
TILE = 512
COLS = 256
LATER = {
    2: (("neighbours", 3), ("own", 5)),
    3: (("neighbours", 4), ("opposite", 3)),
    5: (("neighbours", 5), ("opposite", 4)),
    7: (("opposite", 5),),
}


def dot(a, b):
    return jnp.dot(a, b, preferred_element_type=F32)


def dot_as(a, b, dims):
    return lax.dot_general(a, b, dims, preferred_element_type=F32)


def normed(h):
    wide = h.astype(F32)
    scale = lax.rsqrt(jnp.mean(wide * wide, -1, keepdims=True) + 1e-6)
    return wide, scale


def cuts(n, size):
    return [slice(at, min(at + size, n)) for at in range(0, n, size)]


def whole(shape):
    return pl.BlockSpec(shape, lambda *_: (0,) * len(shape), pipeline_mode=pl.Buffered(1))


def rows_of(width, tile=TILE):
    return pl.BlockSpec((tile, width), lambda i: (i, 0))


def params(**more):
    return pltpu.CompilerParams(dimension_semantics=("arbitrary",), vmem_limit_bytes=VMEM_LIMIT, **more)


def cost(matmuls, rows, d, ff, moved):
    return pl.CostEstimate(flops=2 * matmuls * rows * d * ff, bytes_accessed=moved, transcendentals=0)


class Gather:
    def __init__(self, n, shards, fulls, send, recv, local):
        self.n, self.shards, self.fulls, self.send, self.recv, self.local = n, shards, fulls, send, recv, local
        self.me = lax.axis_index("dp")
        rep = lax.axis_index("rep")
        self.core = lax.rem(rep, 2)
        self.partner = {"rep": rep + 1 - 2 * self.core}
        self.right = {"dp": lax.rem(self.me + 1, n)}
        self.left = {"dp": lax.rem(self.me + n - 1, n)}

    def shard(self, m):
        ref = self.shards[m % 3]
        return ref.at[m // 3]

    def piece(self, m, away, quarter=None):
        block = self.shards[m % 3].shape[1]
        half = block // 2
        at = lax.rem(self.me + away + self.n, self.n) * block + self.core * half
        if quarter is None:
            return self.fulls[m].at[pl.ds(at, half)]
        return self.fulls[m].at[pl.ds(at + quarter * (half // 2), half // 2)]

    def other_piece(self, m, away, quarter=None):
        block = self.shards[m % 3].shape[1]
        half = block // 2
        at = lax.rem(self.me + away + self.n, self.n) * block + (1 - self.core) * half
        if quarter is None:
            return self.fulls[m].at[pl.ds(at, half)]
        return self.fulls[m].at[pl.ds(at + quarter * (half // 2), half // 2)]

    def copy(self, m, k, src, dst, to):
        return pltpu.make_async_remote_copy(
            src_ref=src, dst_ref=dst, send_sem=self.send.at[m, k], recv_sem=self.recv.at[m, k],
            device_id=to, device_id_type=pl.DeviceIdType.MESH,
        )

    def sends(self, m, k):
        if k < 2:
            block = self.shards[m % 3].shape[1]
            src = self.shard(m).at[pl.ds(self.core * (block // 2), block // 2)]
            return self.copy(m, k, src, self.piece(m, 0), (self.right, self.left)[k])
        part = {2: (-1, 0), 3: (1, 1), 4: (-1, None), 5: (1, None), 6: (2, 0), 7: (2, 1)}[k]
        ref = self.piece(m, *part)
        return self.copy(m, k, ref, ref, (self.right, self.left)[k - 2] if k < 4 else self.partner)

    def arrives(self, m, k):
        if k < 4:
            part = ((-1, None), (1, None), (2, 0), (2, 1))[k]
            ref = self.piece(m, *part)
        else:
            part = {4: (-1, None), 5: (1, None), 6: (2, 0), 7: (2, 1)}[k]
            ref = self.other_piece(m, *part)
        return self.copy(m, k, ref, ref, self.partner)

    def mine(self, m):
        block = self.shards[m % 3].shape[1]
        return pltpu.make_async_copy(self.shard(m), self.fulls[m].at[pl.ds(self.me * block, block)], self.local.at[m])

    def greet(self):
        barrier = pltpu.get_barrier_semaphore()
        for other in (self.left, self.right, self.partner):
            pl.semaphore_signal(barrier, inc=1, device_id=other, device_id_type=pl.DeviceIdType.MESH)
        pl.semaphore_wait(barrier, 3)

    def start(self, m, ks):
        for k in ks:
            self.sends(m, k).start()

    def own(self, m):
        self.start(m, (0, 1))
        self.mine(m).start()

    def neighbours(self, m):
        self.arrives(m, 0).wait_recv()
        self.start(m, (2, 4))
        self.arrives(m, 1).wait_recv()
        self.start(m, (3, 5))

    def opposite(self, m):
        self.arrives(m, 2).wait_recv()
        self.start(m, (6,))
        self.arrives(m, 3).wait_recv()
        self.start(m, (7,))

    def complete(self, m):
        self.mine(m).wait()
        for k in range(4, 8):
            self.arrives(m, k).wait_recv()

    def sent(self, m):
        for k in range(8):
            self.sends(m, k).wait_send()


def forward_kernel(n, x, sg, su, sd, h1, act, g_out, u_out, *rest):
    outs, fulls, (send, recv, local, out_sem) = rest[:6], rest[6:12], rest[12:]
    gather = Gather(n, (sg, su, sd), fulls, send, recv, local)
    step = pl.program_id(0)

    def keep(m):
        return pltpu.make_async_copy(fulls[m], outs[m], out_sem.at[m])

    @pl.when(step == 0)
    def _():
        gather.greet()
        gather.own(0)
        gather.own(1)
        gather.neighbours(0)
        gather.own(2)
        gather.neighbours(1)
        gather.opposite(0)
        gather.own(3)
        gather.neighbours(2)
        gather.opposite(1)
        gather.own(4)
        gather.opposite(2)
        for m in range(3):
            gather.complete(m)
            keep(m).start()

    for at, events in LATER.items():
        @pl.when(step == at)
        def _():
            for stage, m in events:
                getattr(gather, stage)(m)

    wg, wu, wd = fulls[:3]
    h = x[...]
    wide, scale = normed(h)
    a = (wide * scale).astype(BF16)
    for s in cuts(wg.shape[1], COLS):
        g = dot(a, wg[:, s])
        u = dot(a, wu[:, s])
        g_out[:, s] = g
        u_out[:, s] = u
        act[:, s] = (g * jax.nn.sigmoid(g) * u).astype(BF16)
    h1[...] = h + dot(act[...], wd[...]).astype(BF16)

    @pl.when(step == pl.num_programs(0) - 1)
    def _():
        for m in range(3, 6):
            gather.complete(m)
            keep(m).start()
        for m in range(6):
            gather.sent(m)
            keep(m).wait()


def forward(n, x, sg, su, sd):
    rows, d = x.shape
    ff = sg.shape[2]
    shapes = [(d, ff), (d, ff), (ff, d)] * 2
    outs = [((rows, d), BF16), ((rows, ff), BF16), ((rows, ff), F32), ((rows, ff), F32)] + [(s, BF16) for s in shapes]
    anywhere = pl.BlockSpec(memory_space=pl.ANY)
    assert rows // TILE == 8 and n == 4
    return pl.pallas_call(
        functools.partial(forward_kernel, n),
        grid=(rows // TILE,),
        out_shape=[jax.ShapeDtypeStruct(*o) for o in outs],
        in_specs=[rows_of(d)] + [anywhere] * 3,
        out_specs=[rows_of(d), rows_of(ff), rows_of(ff), rows_of(ff)] + [anywhere] * 6,
        scratch_shapes=[pltpu.VMEM(s, BF16) for s in shapes]
        + [pltpu.SemaphoreType.DMA((6, 8)), pltpu.SemaphoreType.DMA((6, 8)), pltpu.SemaphoreType.DMA((6,)), pltpu.SemaphoreType.DMA((6,))],
        compiler_params=params(collective_id=0, has_side_effects=True),
        cost_estimate=cost(3, rows, d, ff, 100 * 2**20),
        name="forward",
    )(x, sg, su, sd)


def through_norm(wide, scale, da, dh):
    m = jnp.mean(da * wide, -1, keepdims=True)
    return dh + (scale * da - wide * (scale * scale * scale * m)).astype(BF16)


def gate_grads(g, u, dact):
    sig = jax.nn.sigmoid(g)
    silu = g * sig
    return silu, (dact * u * (sig + silu * (1 - sig))).astype(BF16), (dact * silu).astype(BF16)


def last_kernel(h_ref, dy_ref, wg, wu, wd, dh, act, dg, du):
    wide, scale = normed(h_ref[...])
    a = (wide * scale).astype(BF16)
    dy = dy_ref[...]
    for s in cuts(wg.shape[1], COLS):
        g = dot(a, wg[:, s])
        u = dot(a, wu[:, s])
        dact = dot_as(dy, wd[s, :], NT).astype(BF16).astype(F32)
        silu, dg[:, s], du[:, s] = gate_grads(g, u, dact)
        act[:, s] = (silu * u).astype(BF16)
    da = dot_as(dg[...], wg[...], NT) + dot_as(du[...], wu[...], NT)
    dh[...] = through_norm(wide, scale, da.astype(BF16).astype(F32), dy)


def last(h, dy, wg, wu, wd):
    rows, d = h.shape
    ff = wg.shape[1]
    return pl.pallas_call(
        last_kernel,
        grid=(rows // TILE,),
        out_shape=[jax.ShapeDtypeStruct((rows, d), BF16)] + [jax.ShapeDtypeStruct((rows, ff), BF16)] * 3,
        in_specs=[rows_of(d), rows_of(d)] + [whole(w.shape) for w in (wg, wu, wd)],
        out_specs=[rows_of(d)] + [rows_of(ff)] * 3,
        compiler_params=params(),
        cost_estimate=cost(5, rows, d, ff, 80 * 2**20),
        name="last",
    )(h, dy, wg, wu, wd)


def first_kernel(h_ref, dh1_ref, g_ref, u_ref, wg, wu, wd, dx, dg, du):
    wide, scale = normed(h_ref[...])
    dh1 = dh1_ref[...]
    for s in cuts(wg.shape[1], COLS):
        dact = dot_as(dh1, wd[s, :], NT).astype(BF16).astype(F32)
        _, dg[:, s], du[:, s] = gate_grads(g_ref[:, s], u_ref[:, s], dact)
    da = dot_as(dg[...], wg[...], NT) + dot_as(du[...], wu[...], NT)
    dx[...] = through_norm(wide, scale, da.astype(BF16).astype(F32), dh1)


def first(h, dh1, g, u, wg, wu, wd):
    rows, d = h.shape
    ff = wg.shape[1]
    return pl.pallas_call(
        first_kernel,
        grid=(rows // TILE,),
        out_shape=[jax.ShapeDtypeStruct((rows, d), BF16)] + [jax.ShapeDtypeStruct((rows, ff), BF16)] * 2,
        in_specs=[rows_of(d), rows_of(d), rows_of(ff), rows_of(ff)] + [whole(w.shape) for w in (wg, wu, wd)],
        out_specs=[rows_of(d)] + [rows_of(ff)] * 2,
        compiler_params=params(),
        cost_estimate=cost(3, rows, d, ff, 110 * 2**20),
        name="first",
    )(h, dh1, g, u, wg, wu, wd)


def in_kernel(h_ref, grad_ref, out, total):
    step = pl.program_id(0)

    @pl.when(step == 0)
    def _():
        total[...] = jnp.zeros_like(total)

    wide, scale = normed(h_ref[...])
    a = (wide * scale).astype(BF16)
    for s in cuts(grad_ref.shape[1], COLS):
        total[:, s] += dot_as(a, grad_ref[:, s], TN)

    @pl.when(step == pl.num_programs(0) - 1)
    def _():
        out[...] = total[...].astype(BF16)


def grad_in(h, grad, name, tile=1024):
    rows, d = h.shape
    ff = grad.shape[1]
    return pl.pallas_call(
        in_kernel,
        grid=(rows // tile,),
        out_shape=jax.ShapeDtypeStruct((d, ff), BF16),
        in_specs=[rows_of(d, tile), rows_of(ff, tile)],
        out_specs=whole((d, ff)),
        scratch_shapes=[pltpu.VMEM((d, ff), F32)],
        compiler_params=params(),
        cost_estimate=cost(1, rows, d, ff, 24 * 2**20),
        name=name,
    )(h, grad)


def out_kernel(act_ref, dh_ref, out):
    out[...] = dot_as(act_ref[...], dh_ref[...], TN).astype(BF16)


def grad_out(act, dh, name):
    rows, ff = act.shape
    d = dh.shape[1]
    return pl.pallas_call(
        out_kernel,
        grid=(ff // COLS,),
        out_shape=jax.ShapeDtypeStruct((ff, d), BF16),
        in_specs=[pl.BlockSpec((rows, COLS), lambda i: (0, i)), whole((rows, d))],
        out_specs=pl.BlockSpec((COLS, d), lambda i: (i, 0)),
        compiler_params=params(),
        cost_estimate=cost(1, rows, d, ff, 24 * 2**20),
        name=name,
    )(act, dh)


def solution(mesh):
    n = mesh.shape["dp"]

    def scatter(term):
        return lax.psum_scatter(term, "dp", scatter_dimension=0, tiled=True)

    def body(x, dy, sg, su, sd):
        x, dy = x[0], dy[0]
        h1, act0, g0, u0, wg0, wu0, wd0, wg1, wu1, wd1 = forward(n, x, sg, su, sd)
        dh1, act1, dg1, du1 = last(h1, dy, wg1, wu1, wd1)
        down1 = scatter(grad_out(act1, dy, "down1"))
        gate1 = scatter(grad_in(h1, dg1, "gate1"))
        up1 = scatter(grad_in(h1, du1, "up1"))
        down0 = scatter(grad_out(act0, dh1, "down0"))
        dx, dg0, du0 = first(x, dh1, g0, u0, wg0, wu0, wd0)
        gate0 = scatter(grad_in(x, dg0, "gate0"))
        up0 = scatter(grad_in(x, du0, "up0"))
        return dx[None], jnp.stack([gate0, gate1]), jnp.stack([up0, up1]), jnp.stack([down0, down1])

    tokens = P(("rep", "dp"), None, None)
    return jax.shard_map(
        body,
        mesh=mesh,
        in_specs=(tokens, tokens) + (P(None, "dp", None),) * 3,
        out_specs=(tokens,) + (P("rep", "dp", None),) * 3,
        check_vma=False,
    )
```

time: 677 us -> 416 us (0.61)
  matrix products: 348 us -> 0 us
  Pallas kernels: 0 us -> 338 us
  other arithmetic: 117 us -> 7.53 us
  waiting for transfers between devices: 151 us -> 56.1 us
  local copies, waits for them, and re-layouts: 42.1 us -> 0 us
    dot_general x17 -> x0, matrix products: 348 us -> none  [the longest x6 142 us: layer(): up = jnp.dot(a, w['w_up'], preferred_element_type=jnp.float32)]
    pallas_call x0 -> x9, Pallas kernels: none -> 338 us  [the longest x1 98 us: forward(): pl.pallas_call(functools.partial(forward_kernel, n), grid=(rows // TILE,)...]
    unnamed x18 -> x6, waiting for transfers between devices: 101 us -> 0.32 us
    unnamed x3 -> x0, other arithmetic: 80.6 us -> none
    reduce_scatter x0 -> x6, waiting for transfers between devices: none -> 55.8 us  [scatter(): return lax.psum_scatter(term, 'dp', scatter_dimension=0, tiled=True)]
    squeeze x6 -> x0, waiting for transfers between devices: 49.5 us -> none  [stack(): h = layer(h, {name: w[number] for name, w in weights.items()})]
    unnamed x27 -> x0, local copies, waits for them, and re-layouts: 34.7 us -> none
    reshape x4 -> x0, other arithmetic: 14.6 us -> none  [the longest x1 11.1 us: step(): by_x.reshape(shape)]
  transfers between devices with their start and end apart: 12 -> 6, of which waited for: 7 -> 2; matrix products, arithmetic and copies ran while one was open for 58% -> 1% of each run, Pallas kernels for 0% -> 35%
where the time goes in v1:
time: 416 us
  Pallas kernels  338 us (81%)
  waiting for transfers between devices  56.1 us (13%)
  between operations  14.2 us (3%)
  other arithmetic  7.53 us (2%)
    pallas_call x1, Pallas kernels, forward(): pl.pallas_call(functools.partial(forward_kernel, n), grid=(rows // TILE,)...  98 us
    pallas_call x1, Pallas kernels, last(): pl.pallas_call(last_kernel, grid=(rows // TILE,), out_shape=[jax.ShapeDty...  76.8 us
    pallas_call x4, Pallas kernels, grad_in(): pl.pallas_call(in_kernel, grid=(rows // tile,), out_shape=jax.ShapeDtypeS...  73.4 us
    reduce_scatter x6, waiting for transfers between devices, scatter(): return lax.psum_scatter(term, 'dp', scatter_dimension=0, tiled=True)  55.8 us
    pallas_call x1, Pallas kernels, first(): pl.pallas_call(first_kernel, grid=(rows // TILE,), out_shape=[jax.ShapeDt...  55.6 us
    pallas_call x2, Pallas kernels, grad_out(): pl.pallas_call(out_kernel, grid=(ff // COLS,), out_shape=jax.ShapeDtypeSt...  34.3 us
  transfers between devices with their start and end apart: 6, of which 2 were waited for; matrix products, arithmetic and copies ran while one was open for 1% of the time, Pallas kernels for 35%

profile of v1, /device:TPU:112, one launch (start us, length us, event | category | flops | bytes accessed | tf_op | source)
XLA Modules:
  0.0 416.2 jit_solution(2469448810375962320)
XLA Ops:
  7.2 0.1 reduce-scatter.15.cloned.1.call-start
  7.2 98.0 %forward.1 = (bf16[4096,768]{1,0:T(8,128)(2,1)}, bf16[4096,1792]{1,0:T(8,128)(2,1)}, f32[4096,1792]{1,0:T(8,128)}, f32[4096,1792]{1,0:T(8,128)}, bf16[768,1792]{...) custom-call(bf16[4096,768]{1,0:T(8,128)(2,1)} %bitcast.17, ...), custom_call_target="tpu_custom_call" | custom-call | flops 33822867456 | bytes 104857600 | tf_op jit(solution)/shard_map/forward/pallas_call | solution.py:213
  105.2 76.8 %last.1 = (bf16[4096,768]{1,0:T(8,128)(2,1)}, bf16[4096,1792]{1,0:T(8,128)(2,1)}, bf16[4096,1792]{1,0:T(8,128)(2,1)}, bf16[4096,1792]{1,0:T(8,128)(2,1)}) custom-call(bf16[4096,768]{1,0:T(8,128)(2,1)} %get-tuple-element.21.h_ref, bf16[4096,768]{1,0:T(8,128)(2,1)} %bitcast.15, bf16[768,1792]{1,0:T(8,128)(2,1)} %get-tuple-element.22.wg, ...), custom_call_target="tpu_custom_call" | custom-call | flops 56371445760 | bytes 83886080 | tf_op jit(solution)/shard_map/last/pallas_call | solution.py:255
  182.0 17.2 %down0.1 = bf16[1792,768]{1,0:T(8,128)(2,1)} custom-call(bf16[4096,1792]{1,0:T(8,128)(2,1)} %get-tuple-element.36.act_ref, bf16[4096,768]{1,0:T(8,128)(2,1)} %get-tuple-element.25.dh1_ref.dh_ref), custom_call_target="tpu_custom_call" | custom-call | flops 11274289152 | bytes 25165824 | tf_op jit(solution)/shard_map/down0/pallas_call | solution.py:332
  199.2 0.1 reduce-scatter.15.cloned.1.call-update
  199.3 0.1 reduce-scatter.17.cloned.1.call-start
  199.3 17.2 %down1.1 = bf16[1792,768]{1,0:T(8,128)(2,1)} custom-call(bf16[4096,1792]{1,0:T(8,128)(2,1)} %get-tuple-element.37.act_ref, bf16[4096,768]{1,0:T(8,128)(2,1)} %bitcast.16), custom_call_target="tpu_custom_call" | custom-call | flops 11274289152 | bytes 25165824 | tf_op jit(solution)/shard_map/down1/pallas_call | solution.py:332
  216.5 0.1 reduce-scatter.17.cloned.1.call-update
  216.6 0.1 reduce-scatter.13.cloned.1.call-start
  216.6 18.5 %up1.1 = bf16[768,1792]{1,0:T(8,128)(2,1)} custom-call(bf16[4096,768]{1,0:T(8,128)(2,1)} %get-tuple-element.21.h_ref, bf16[4096,1792]{1,0:T(8,128)(2,1)} %get-tuple-element.35.grad_ref), custom_call_target="tpu_custom_call" | custom-call | flops 11274289152 | bytes 25165824 | tf_op jit(solution)/shard_map/up1/pallas_call | solution.py:312
  235.1 0.1 reduce-scatter.13.cloned.1.call-update
  235.2 0.1 reduce-scatter.11.cloned.1.call-start
  235.2 55.6 %first.1 = (bf16[4096,768]{1,0:T(8,128)(2,1)}, bf16[4096,1792]{1,0:T(8,128)(2,1)}, bf16[4096,1792]{1,0:T(8,128)(2,1)}) custom-call(bf16[4096,768]{1,0:T(8,128)(2,1)} %bitcast.18, bf16[4096,768]{1,0:T(8,128)(2,1)} %get-tuple-element.25.dh1_ref.dh_ref, f32[4096,1792]{1,0:T(8,128)} %get-tuple-element.26.g_ref, f32[4096,1792]{1,0:T(8,128)} %get-tuple-element.27.u_ref, ...), custom_call_target="tpu_custom_call" | custom-call | flops 33822867456 | bytes 115343360 | tf_op jit(solution)/shard_map/first/pallas_call | solution.py:280
  290.8 18.2 %up0.1 = bf16[768,1792]{1,0:T(8,128)(2,1)} custom-call(bf16[4096,768]{1,0:T(8,128)(2,1)} %bitcast.19, bf16[4096,1792]{1,0:T(8,128)(2,1)} %get-tuple-element.34.grad_ref), custom_call_target="tpu_custom_call" | custom-call | flops 11274289152 | bytes 25165824 | tf_op jit(solution)/shard_map/up0/pallas_call | solution.py:312
  309.1 0.1 reduce-scatter.7.cloned.1.call-start
  309.1 18.5 %gate0.1 = bf16[768,1792]{1,0:T(8,128)(2,1)} custom-call(bf16[4096,768]{1,0:T(8,128)(2,1)} %bitcast.20, bf16[4096,1792]{1,0:T(8,128)(2,1)} %get-tuple-element.32.grad_ref), custom_call_target="tpu_custom_call" | custom-call | flops 11274289152 | bytes 25165824 | tf_op jit(solution)/shard_map/gate0/pallas_call | solution.py:312
  327.7 0.1 reduce-scatter.9.cloned.1.call-start
  327.8 18.2 %gate1.1 = bf16[768,1792]{1,0:T(8,128)(2,1)} custom-call(bf16[4096,768]{1,0:T(8,128)(2,1)} %get-tuple-element.21.h_ref, bf16[4096,1792]{1,0:T(8,128)(2,1)} %get-tuple-element.33.grad_ref), custom_call_target="tpu_custom_call" | custom-call | flops 11274289152 | bytes 25165824 | tf_op jit(solution)/shard_map/gate1/pallas_call | solution.py:312
  346.0 0.1 reduce-scatter.9.cloned.1.call-update
  346.1 2.5 pad_maximum_fusion.2
  348.6 2.5 pad_maximum_fusion.1
  351.1 22.9 %reduce-scatter.7.cloned.1.call-done = bf16[192,1792]{1,0:T(8,128)(2,1)} async-done(((bf16[768,1792]{1,0:T(8,128)(2,1)}), bf16[192,1792]{1,0:T(8,128)(2,1)}) %reduce-scatter.7.cloned.1.call-update) | async-done | bytes 688144 | tf_op jit(solution)/shard_map/reduce_scatter | solution.py:348
  374.0 32.9 %reduce-scatter.9.cloned.1.call-done = bf16[192,1792]{1,0:T(8,128)(2,1)} async-done(((bf16[768,1792]{1,0:T(8,128)(2,1)}), bf16[192,1792]{1,0:T(8,128)(2,1)}) %reduce-scatter.9.cloned.1.call-update) | async-done | bytes 688144 | tf_op jit(solution)/shard_map/reduce_scatter | solution.py:348
  406.9 2.5 pad_maximum_fusion
  (6 shorter events, 0.1 us)
Async XLA Ops:
  7.2 338.9 %reduce-scatter.15.cloned.1.call-start = ((), (), s32[]{:S(2)}) async-start(), calls=%async_computation.10 | async-start | bytes 3440640 | tf_op jit(solution)/shard_map/reduce_scatter | solution.py:348
  199.3 146.8 %reduce-scatter.17.cloned.1.call-start = ((), (), s32[]{:S(2)}) async-start(), calls=%async_computation.11 | async-start | bytes 3440640 | tf_op jit(solution)/shard_map/reduce_scatter | solution.py:348
  216.6 132.0 %reduce-scatter.13.cloned.1.call-start = ((), (), s32[]{:S(2)}) async-start(), calls=%async_computation.9 | async-start | bytes 3440640 | tf_op jit(solution)/shard_map/reduce_scatter | solution.py:348
  235.2 113.5 %reduce-scatter.11.cloned.1.call-start = ((), (), s32[]{:S(2)}) async-start(), calls=%async_computation.8 | async-start | bytes 3440640 | tf_op jit(solution)/shard_map/reduce_scatter | solution.py:348
  309.1 64.9 %reduce-scatter.7.cloned.1.call-start = ((), (), s32[]{:S(2)}) async-start(), calls=%async_computation.6 | async-start | bytes 3440640 | tf_op jit(solution)/shard_map/reduce_scatter | solution.py:348
  327.7 79.2 %reduce-scatter.9.cloned.1.call-start = ((), (), s32[]{:S(2)}) async-start(), calls=%async_computation.7 | async-start | bytes 3440640 | tf_op jit(solution)/shard_map/reduce_scatter | solution.py:348
Sparse Core Ops, SparseCore 0:
  199.4 31.8 reduce-scatter.14
  233.6 30.6 reduce-scatter.16
  266.6 30.6 reduce-scatter.12
  309.2 31.8 reduce-scatter.10
  343.3 30.6 reduce-scatter.6
  376.2 30.6 reduce-scatter.8

commit v2 on v1

--- a/solution.py
+++ b/solution.py
@@ -13,6 +13,8 @@
 VMEM_LIMIT = 60 * 2**20
 TILE = 512
 COLS = 256
+SMALL = 256
+SLOTS = 6
 LATER = {
     2: (("neighbours", 3), ("own", 5)),
     3: (("neighbours", 4), ("opposite", 3)),
@@ -149,7 +151,7 @@
             self.sends(m, k).wait_send()
 
 
-def forward_kernel(n, x, sg, su, sd, h1, act, g_out, u_out, *rest):
+def forward_kernel(n, x, sg, su, sd, h1, a_out, act, g_out, u_out, *rest):
     outs, fulls, (send, recv, local, out_sem) = rest[:6], rest[6:12], rest[12:]
     gather = Gather(n, (sg, su, sd), fulls, send, recv, local)
     step = pl.program_id(0)
@@ -185,6 +187,7 @@
     h = x[...]
     wide, scale = normed(h)
     a = (wide * scale).astype(BF16)
+    a_out[...] = a
     for s in cuts(wg.shape[1], COLS):
         g = dot(a, wg[:, s])
         u = dot(a, wu[:, s])
@@ -207,7 +210,7 @@
     rows, d = x.shape
     ff = sg.shape[2]
     shapes = [(d, ff), (d, ff), (ff, d)] * 2
-    outs = [((rows, d), BF16), ((rows, ff), BF16), ((rows, ff), F32), ((rows, ff), F32)] + [(s, BF16) for s in shapes]
+    outs = [((rows, d), BF16), ((rows, d), BF16), ((rows, ff), BF16), ((rows, ff), F32), ((rows, ff), F32)] + [(s, BF16) for s in shapes]
     anywhere = pl.BlockSpec(memory_space=pl.ANY)
     assert rows // TILE == 8 and n == 4
     return pl.pallas_call(
@@ -215,7 +218,7 @@
         grid=(rows // TILE,),
         out_shape=[jax.ShapeDtypeStruct(*o) for o in outs],
         in_specs=[rows_of(d)] + [anywhere] * 3,
-        out_specs=[rows_of(d), rows_of(ff), rows_of(ff), rows_of(ff)] + [anywhere] * 6,
+        out_specs=[rows_of(d), rows_of(d), rows_of(ff), rows_of(ff), rows_of(ff)] + [anywhere] * 6,
         scratch_shapes=[pltpu.VMEM(s, BF16) for s in shapes]
         + [pltpu.SemaphoreType.DMA((6, 8)), pltpu.SemaphoreType.DMA((6, 8)), pltpu.SemaphoreType.DMA((6,)), pltpu.SemaphoreType.DMA((6,))],
         compiler_params=params(collective_id=0, has_side_effects=True),
@@ -235,9 +238,10 @@
     return silu, (dact * u * (sig + silu * (1 - sig))).astype(BF16), (dact * silu).astype(BF16)
 
 
-def last_kernel(h_ref, dy_ref, wg, wu, wd, dh, act, dg, du):
+def last_kernel(h_ref, dy_ref, wg, wu, wd, dh, a_out, act, dg, du):
     wide, scale = normed(h_ref[...])
     a = (wide * scale).astype(BF16)
+    a_out[...] = a
     dy = dy_ref[...]
     for s in cuts(wg.shape[1], COLS):
         g = dot(a, wg[:, s])
@@ -255,109 +259,426 @@
     return pl.pallas_call(
         last_kernel,
         grid=(rows // TILE,),
-        out_shape=[jax.ShapeDtypeStruct((rows, d), BF16)] + [jax.ShapeDtypeStruct((rows, ff), BF16)] * 3,
+        out_shape=[jax.ShapeDtypeStruct((rows, d), BF16)] * 2 + [jax.ShapeDtypeStruct((rows, ff), BF16)] * 3,
         in_specs=[rows_of(d), rows_of(d)] + [whole(w.shape) for w in (wg, wu, wd)],
-        out_specs=[rows_of(d)] + [rows_of(ff)] * 3,
+        out_specs=[rows_of(d)] * 2 + [rows_of(ff)] * 3,
         compiler_params=params(),
         cost_estimate=cost(5, rows, d, ff, 80 * 2**20),
         name="last",
     )(h, dy, wg, wu, wd)
 
 
-def first_kernel(h_ref, dh1_ref, g_ref, u_ref, wg, wu, wd, dx, dg, du):
-    wide, scale = normed(h_ref[...])
-    dh1 = dh1_ref[...]
-    for s in cuts(wg.shape[1], COLS):
-        dact = dot_as(dh1, wd[s, :], NT).astype(BF16).astype(F32)
-        _, dg[:, s], du[:, s] = gate_grads(g_ref[:, s], u_ref[:, s], dact)
-    da = dot_as(dg[...], wg[...], NT) + dot_as(du[...], wu[...], NT)
-    dx[...] = through_norm(wide, scale, da.astype(BF16).astype(F32), dh1)
-
-
-def first(h, dh1, g, u, wg, wu, wd):
-    rows, d = h.shape
-    ff = wg.shape[1]
+class Scatter:
+    def __init__(self, n, rows, keep, s1, r1, s2, r2, send, recv):
+        self.rows, self.keep, self.s1, self.r1, self.s2, self.r2, self.send, self.recv = rows, keep, s1, r1, s2, r2, send, recv
+        self.n = n
+        self.me = lax.axis_index("dp")
+        self.right = {"dp": lax.rem(self.me + 1, n)}
+        self.left = {"dp": lax.rem(self.me + n - 1, n)}
+
+    def copy(self, slot, k, src, dst):
+        return pltpu.make_async_remote_copy(
+            src_ref=src, dst_ref=dst, send_sem=self.send.at[slot, k], recv_sem=self.recv.at[slot, k],
+            device_id=self.left if k % 2 else self.right, device_id_type=pl.DeviceIdType.MESH,
+        )
+
+    def opposites(self, slot, k):
+        half = self.rows // 2
+        return self.copy(slot, k, self.s1.at[slot, pl.ds(k * half, half)], self.r1.at[slot, k])
+
+    def sums(self, slot, k):
+        return self.copy(slot, 2 + k, self.s2.at[slot, k], self.r2.at[slot, k])
+
+    def of(self, term, away):
+        at = pl.multiple_of(lax.rem(self.me + away, self.n) * self.rows, 64)
+        return term[pl.ds(at, self.rows), :]
+
+    def put(self, slot, term):
+        self.s1[slot] = self.of(term, 2).astype(BF16)
+        self.keep[slot, 0] = self.of(term, 1)
+        self.keep[slot, 1] = self.of(term, self.n - 1)
+        self.keep[slot, 2] = self.of(term, 0)
+
+    def begin(self, slot):
+        for k in range(2):
+            self.opposites(slot, k).start()
+
+    def middle(self, slot):
+        half = self.rows // 2
+        for k in range(2):
+            self.opposites(slot, k).wait_recv()
+        for k in range(2):
+            with_theirs, alone = pl.ds(k * half, half), pl.ds((1 - k) * half, half)
+            self.s2[slot, k, with_theirs] = (self.keep[slot, k, with_theirs] + self.r1[slot, k].astype(F32)).astype(BF16)
+            self.s2[slot, k, alone] = self.keep[slot, k, alone].astype(BF16)
+        for k in range(2):
+            self.sums(slot, k).start()
+
+    def end(self, slot):
+        for k in range(2):
+            self.sums(slot, k).wait_recv()
+        out = self.keep[slot, 2] + self.r2[slot, 0].astype(F32) + self.r2[slot, 1].astype(F32)
+        for k in range(2):
+            self.opposites(slot, k).wait_send()
+            self.sums(slot, k).wait_send()
+        return out.astype(BF16)
+
+
+def backward_kernel(
+    n, dims, dy, dh1, x, a0, a1, act0, act1, dg1, du1, g0, u0, wg0, wu0, wd0,
+    wide_out, down_out, dx, dg0, du0,
+    ra, ract, blk, term, wd, g_t, u_t, dh_t, dg_t, du_t, x_t, dx_t,
+    wk, ws1, wr1, ws2, wr2, dk, ds1, dr1, ds2, dr2,
+    wsend, wrecv, dsend, drecv, blk_sem, res_sem, in_sem, out_sem,
+):
+    rows, d, ff = dims
+    tiles = rows // SMALL
+    wides, downs = ff // COLS, d // COLS
+    first_tiles = tiles // 2 - downs
+    wide = Scatter(n, d // n, wk, ws1, wr1, ws2, wr2, wsend, wrecv)
+    down = Scatter(n, ff // n, dk, ds1, dr1, ds2, dr2, dsend, drecv)
+
+    def resident(src, dst, k):
+        return pltpu.make_async_copy(src, dst, res_sem.at[k])
+
+    load_a1 = lambda: resident(a1, ra, 0)
+    load_a0 = lambda: resident(a0, ra, 0)
+    load_act1 = lambda: resident(act1, ract, 1)
+    load_act0 = lambda: resident(act0, ract, 1)
+    load_wd = lambda: resident(wd0, wd, 2)
+    load_wg = lambda: resident(wg0, ract.at[pl.ds(0, d)], 1)
+    load_wu = lambda: resident(wu0, ract.at[pl.ds(d, d)], 2)
+
+    def column(src, j, slot):
+        return pltpu.make_async_copy(src.at[:, pl.ds(pl.multiple_of(j * COLS, COLS), COLS)], blk.at[slot], blk_sem.at[slot])
+
+    def load_wide(r, i, slot):
+        for at, src in ((0, dg1), (1, du1)):
+            @pl.when(r == at)
+            def _():
+                column(src, i, slot).start()
+
+    def load_down(r, j, slot):
+        for at, src in ((0, dy), (1, dh1)):
+            @pl.when(r == at)
+            def _():
+                column(src, j, slot).start()
+
+    def load_last(i, slot):
+        @pl.when(i < wides)
+        def _():
+            column(dg0, i, slot).start()
+
+        @pl.when(i >= wides)
+        def _():
+            column(du0, i - wides, slot).start()
+
+    def tile_of(ref, t):
+        return ref.at[pl.ds(pl.multiple_of(t * SMALL, SMALL), SMALL)]
+
+    def tile_in(t):
+        slot = lax.rem(t, 2)
+        return [pltpu.make_async_copy(tile_of(src, t), dst.at[slot], in_sem.at[k, slot]) for k, (src, dst) in enumerate(((g0, g_t), (u0, u_t), (dh1, dh_t)))]
+
+    def tile_out(t):
+        slot = lax.rem(t, 2)
+        return [pltpu.make_async_copy(src.at[slot], tile_of(dst, t), out_sem.at[k, slot]) for k, (src, dst) in enumerate(((dg_t, dg0), (du_t, du0)))]
+
+    def tile(t):
+        slot = lax.rem(t, 2)
+        for c in tile_in(t):
+            c.wait()
+
+        @pl.when(t + 1 < tiles)
+        def _():
+            for c in tile_in(t + 1):
+                c.start()
+
+        @pl.when(t >= 2)
+        def _():
+            for c in tile_out(t - 2):
+                c.wait()
+
+        dh = dh_t[slot]
+        for s in cuts(ff, COLS):
+            dact = dot_as(dh, wd[s, :], NT).astype(BF16).astype(F32)
+            _, dg_t[slot, :, s], du_t[slot, :, s] = gate_grads(g_t[slot, :, s], u_t[slot, :, s], dact)
+        for c in tile_out(t):
+            c.start()
+
+    def late_in(t):
+        slot = lax.rem(t, 2)
+        pairs = ((dg0, dg_t), (du0, du_t), (dh1, dh_t), (x, x_t))
+        return [pltpu.make_async_copy(tile_of(src, t), dst.at[slot], in_sem.at[k, slot]) for k, (src, dst) in enumerate(pairs)]
+
+    def late_out(t):
+        slot = lax.rem(t, 2)
+        return pltpu.make_async_copy(dx_t.at[slot], tile_of(dx, t), out_sem.at[0, slot])
+
+    def late(t):
+        slot = lax.rem(t, 2)
+        for c in late_in(t):
+            c.wait()
+
+        @pl.when(t + 1 < tiles)
+        def _():
+            for c in late_in(t + 1):
+                c.start()
+
+        @pl.when(t >= 2)
+        def _():
+            late_out(t - 2).wait()
+
+        h, scale = normed(x_t[slot])
+        da = dot_as(dg_t[slot], ract[0:d, :], NT) + dot_as(du_t[slot], ract[d : 2 * d, :], NT)
+        dx_t[slot] = through_norm(h, scale, da.astype(BF16).astype(F32), dh_t[slot])
+        late_out(t).start()
+
+    def end_wide(k):
+        wide_out[k // wides, :, pl.ds(pl.multiple_of(lax.rem(k, wides) * COLS, COLS), COLS)] = wide.end(lax.rem(k, SLOTS))
+
+    def end_down(r, j):
+        down_out[r, :, pl.ds(pl.multiple_of(j * COLS, COLS), COLS)] = down.end(j)
+
+    def due_wide(r, i):
+        k = wides * r + i
+
+        @pl.when(i >= 2)
+        def _():
+            wide.middle(lax.rem(k + SLOTS - 2, SLOTS))
+
+        @pl.when((r >= 1) & (i < 2))
+        def _():
+            down.middle(i + downs - 2)
+
+        @pl.when(i >= 4)
+        def _():
+            end_wide(k - 4)
+
+        @pl.when((r >= 1) & (i == 0))
+        def _():
+            end_wide(k - 1)
+
+        @pl.when((r >= 1) & (i >= 1) & (i < 4))
+        def _():
+            end_down(r - 1, i - 1)
+
+    def due_down(r, j):
+        k = wides * r + wides + j
+
+        @pl.when(j < 2)
+        def _():
+            wide.middle(lax.rem(k - 2, SLOTS))
+
+        @pl.when(j == 2)
+        def _():
+            down.middle(0)
+
+        end_wide(k - 4)
+
+    def wide_step(r, i, slot, tail):
+        term[0:d, :] = dot_as(ra[...], blk[slot], TN)
+        k = lax.rem(wides * r + i, SLOTS)
+        wide.put(k, term)
+        due_wide(r, i)
+        tail()
+        wide.begin(k)
+
+    load_a1().start()
+    load_wide(0, 0, 0)
+    load_wd().start()
+    for c in tile_in(0):
+        c.start()
+    load_act1().start()
+    barrier = pltpu.get_barrier_semaphore()
+    for other in (wide.left, wide.right):
+        pl.semaphore_signal(barrier, inc=1, device_id=other, device_id_type=pl.DeviceIdType.MESH)
+    pl.semaphore_wait(barrier, 2)
+    load_a1().wait()
+    load_wd().wait()
+
+    def round_(r, _):
+        def wide_block(i, _):
+            q = (wides + downs) * r + i
+            slot = lax.rem(q, 2)
+            column(dg1, 0, slot).wait()
+
+            @pl.when(i + 1 < wides)
+            def _():
+                load_wide(r, i + 1, 1 - slot)
+
+            @pl.when(i + 1 == wides)
+            def _():
+                load_down(r, 0, 1 - slot)
+
+            def tail():
+                at = (i * first_tiles) // wides
+
+                @pl.when(((i + 1) * first_tiles) // wides > at)
+                def _():
+                    tile(r * (tiles // 2) + at)
+
+            wide_step(r, i, slot, tail)
+            return 0
+
+        lax.fori_loop(0, wides, wide_block, 0)
+
+        @pl.when(r == 1)
+        def _():
+            load_a0().start()
+
+        load_act1().wait()
+
+        def down_block(j, _):
+            q = (wides + downs) * r + wides + j
+            slot = lax.rem(q, 2)
+            column(dy, 0, slot).wait()
+
+            @pl.when(j + 1 < downs)
+            def _():
+                load_down(r, j + 1, 1 - slot)
+
+            @pl.when((j + 1 == downs) & (r == 0))
+            def _():
+                load_wide(r + 1, 0, 1 - slot)
+
+            for s in cuts(ff, ff // 2):
+                term[s, :] = dot_as(ract[:, s], blk[slot], TN)
+            down.put(j, term)
+            due_down(r, j)
+            tile(r * (tiles // 2) + first_tiles + j)
+            down.begin(j)
+            return 0
+
+        lax.fori_loop(0, downs, down_block, 0)
+
+        @pl.when(r == 0)
+        def _():
+            load_act0().start()
+
+        return 0
+
+    lax.fori_loop(0, 2, round_, 0)
+
+    for t in (tiles - 2, tiles - 1):
+        for c in tile_out(t):
+            c.wait()
+    last_q = 2 * (wides + downs)
+    load_last(0, last_q % 2)
+    load_wg().start()
+    load_wu().start()
+    for c in late_in(0):
+        c.start()
+    load_a0().wait()
+    load_wg().wait()
+    load_wu().wait()
+    blocks = 2 * wides
+    late_early = tiles // 2
+
+    def last_block(i, _):
+        slot = lax.rem(last_q + i, 2)
+        column(dg0, 0, slot).wait()
+
+        @pl.when(i + 1 < blocks)
+        def _():
+            load_last(i + 1, 1 - slot)
+
+        def tail():
+            at = (i * late_early) // blocks
+
+            @pl.when(((i + 1) * late_early) // blocks > at)
+            def _():
+                late(at)
+
+        wide_step(2, i, slot, tail)
+        return 0
+
+    lax.fori_loop(0, blocks, last_block, 0)
+
+    def rest(v, _):
+        k = 2 * wides + blocks + v
+
+        def pair(p, _):
+            late(late_early + 2 * v + p)
+            return 0
+
+        lax.fori_loop(0, 2, pair, 0)
+
+        @pl.when(v < 2)
+        def _():
+            wide.middle(lax.rem(k - 2, SLOTS))
+
+        end_wide(k - 4)
+        return 0
+
+    lax.fori_loop(0, 4, rest, 0)
+    for t in (tiles - 2, tiles - 1):
+        late_out(t).wait()
+
+
+def backward(n, dy, dh1, x, a0, a1, act0, act1, dg1, du1, g0, u0, wg0, wu0, wd0):
+    rows, d = dy.shape
+    ff = act1.shape[1]
+    wide, down = d // n, ff // n
+    assert n == 4 and rows // SMALL == 16 and d == 3 * COLS and ff == 7 * COLS
+    anywhere = pl.BlockSpec(memory_space=pl.ANY)
+    inside = pl.BlockSpec(memory_space=pltpu.VMEM)
+
+    def slots(count, chunk):
+        return [
+            pltpu.VMEM((count, 3, chunk, COLS), F32),
+            pltpu.VMEM((count, chunk, COLS), BF16),
+            pltpu.VMEM((count, 2, chunk // 2, COLS), BF16),
+            pltpu.VMEM((count, 2, chunk, COLS), BF16),
+            pltpu.VMEM((count, 2, chunk, COLS), BF16),
+        ]
+
+    dma = pltpu.SemaphoreType.DMA
     return pl.pallas_call(
-        first_kernel,
-        grid=(rows // TILE,),
-        out_shape=[jax.ShapeDtypeStruct((rows, d), BF16)] + [jax.ShapeDtypeStruct((rows, ff), BF16)] * 2,
-        in_specs=[rows_of(d), rows_of(d), rows_of(ff), rows_of(ff)] + [whole(w.shape) for w in (wg, wu, wd)],
-        out_specs=[rows_of(d)] + [rows_of(ff)] * 2,
-        compiler_params=params(),
-        cost_estimate=cost(3, rows, d, ff, 110 * 2**20),
-        name="first",
-    )(h, dh1, g, u, wg, wu, wd)
-
-
-def in_kernel(h_ref, grad_ref, out, total):
-    step = pl.program_id(0)
-
-    @pl.when(step == 0)
-    def _():
-        total[...] = jnp.zeros_like(total)
-
-    wide, scale = normed(h_ref[...])
-    a = (wide * scale).astype(BF16)
-    for s in cuts(grad_ref.shape[1], COLS):
-        total[:, s] += dot_as(a, grad_ref[:, s], TN)
-
-    @pl.when(step == pl.num_programs(0) - 1)
-    def _():
-        out[...] = total[...].astype(BF16)
-
-
-def grad_in(h, grad, name, tile=1024):
-    rows, d = h.shape
-    ff = grad.shape[1]
-    return pl.pallas_call(
-        in_kernel,
-        grid=(rows // tile,),
-        out_shape=jax.ShapeDtypeStruct((d, ff), BF16),
-        in_specs=[rows_of(d, tile), rows_of(ff, tile)],
-        out_specs=whole((d, ff)),
-        scratch_shapes=[pltpu.VMEM((d, ff), F32)],
-        compiler_params=params(),
-        cost_estimate=cost(1, rows, d, ff, 24 * 2**20),
-        name=name,
-    )(h, grad)
-
-
-def out_kernel(act_ref, dh_ref, out):
-    out[...] = dot_as(act_ref[...], dh_ref[...], TN).astype(BF16)
-
-
-def grad_out(act, dh, name):
-    rows, ff = act.shape
-    d = dh.shape[1]
-    return pl.pallas_call(
-        out_kernel,
-        grid=(ff // COLS,),
-        out_shape=jax.ShapeDtypeStruct((ff, d), BF16),
-        in_specs=[pl.BlockSpec((rows, COLS), lambda i: (0, i)), whole((rows, d))],
-        out_specs=pl.BlockSpec((COLS, d), lambda i: (i, 0)),
-        compiler_params=params(),
-        cost_estimate=cost(1, rows, d, ff, 24 * 2**20),
-        name=name,
-    )(act, dh)
+        functools.partial(backward_kernel, n, (rows, d, ff)),
+        out_shape=[
+            jax.ShapeDtypeStruct((4, wide, ff), BF16),
+            jax.ShapeDtypeStruct((2, down, d), BF16),
+            jax.ShapeDtypeStruct((rows, d), BF16),
+            jax.ShapeDtypeStruct((rows, ff), BF16),
+            jax.ShapeDtypeStruct((rows, ff), BF16),
+        ],
+        in_specs=[anywhere] * 14,
+        out_specs=[inside, inside, anywhere, anywhere, anywhere],
+        scratch_shapes=[
+            pltpu.VMEM((rows, d), BF16),
+            pltpu.VMEM((rows, ff), BF16),
+            pltpu.VMEM((2, rows, COLS), BF16),
+            pltpu.VMEM((ff, COLS), F32),
+            pltpu.VMEM((ff, d), BF16),
+            pltpu.VMEM((2, SMALL, ff), F32),
+            pltpu.VMEM((2, SMALL, ff), F32),
+            pltpu.VMEM((2, SMALL, d), BF16),
+            pltpu.VMEM((2, SMALL, ff), BF16),
+            pltpu.VMEM((2, SMALL, ff), BF16),
+            pltpu.VMEM((2, SMALL, d), BF16),
+            pltpu.VMEM((2, SMALL, d), BF16),
+            *slots(SLOTS, wide),
+            *slots(3, down),
+            dma((SLOTS, 4)), dma((SLOTS, 4)), dma((3, 4)), dma((3, 4)),
+            dma((2,)), dma((3,)), dma((4, 2)), dma((2, 2)),
+        ],
+        compiler_params=pltpu.CompilerParams(vmem_limit_bytes=67043328, collective_id=1, has_side_effects=True),
+        cost_estimate=cost(9, rows, d, ff, 300 * 2**20),
+        name="backward",
+    )(dy, dh1, x, a0, a1, act0, act1, dg1, du1, g0, u0, wg0, wu0, wd0)
 
 
 def solution(mesh):
     n = mesh.shape["dp"]
 
-    def scatter(term):
-        return lax.psum_scatter(term, "dp", scatter_dimension=0, tiled=True)
-
     def body(x, dy, sg, su, sd):
         x, dy = x[0], dy[0]
-        h1, act0, g0, u0, wg0, wu0, wd0, wg1, wu1, wd1 = forward(n, x, sg, su, sd)
-        dh1, act1, dg1, du1 = last(h1, dy, wg1, wu1, wd1)
-        down1 = scatter(grad_out(act1, dy, "down1"))
-        gate1 = scatter(grad_in(h1, dg1, "gate1"))
-        up1 = scatter(grad_in(h1, du1, "up1"))
-        down0 = scatter(grad_out(act0, dh1, "down0"))
-        dx, dg0, du0 = first(x, dh1, g0, u0, wg0, wu0, wd0)
-        gate0 = scatter(grad_in(x, dg0, "gate0"))
-        up0 = scatter(grad_in(x, du0, "up0"))
+        h1, a0, act0, g0, u0, wg0, wu0, wd0, wg1, wu1, wd1 = forward(n, x, sg, su, sd)
+        dh1, a1, act1, dg1, du1 = last(h1, dy, wg1, wu1, wd1)
+        wide, down, dx, _, _ = backward(n, dy, dh1, x, a0, a1, act0, act1, dg1, du1, g0, u0, wg0, wu0, wd0)
+        gate1, up1, gate0, up0 = wide
+        down1, down0 = down
         return dx[None], jnp.stack([gate0, gate1]), jnp.stack([up0, up1]), jnp.stack([down0, down1])
 
     tokens = P(("rep", "dp"), None, None)

time: 416 us -> 355 us (0.85)
  waiting for transfers between devices: 56.1 us -> 0 us
  between operations: 14.2 us -> 0.68 us
  Pallas kernels: 338 us -> 346 us
  local copies, waits for them, and re-layouts: 0 us -> 5.68 us
  other arithmetic: 7.53 us -> 2.97 us
    reduce_scatter x6 -> x0, waiting for transfers between devices: 55.8 us -> none  [scatter(): return lax.psum_scatter(term, 'dp', scatter_dimension=0, tiled=True)]
    pallas_call x7 -> x1, Pallas kernels: 163 us -> 170 us  [backward(): pl.pallas_call(functools.partial(backward_kernel, n, (rows, d, ff)), out_...]
  transfers between devices with their start and end apart: 6 -> 0, of which waited for: 2 -> 0; matrix products, arithmetic and copies ran while one was open for 1% -> 0% of each run, Pallas kernels for 35% -> 0%
where the time goes in v2:
time: 355 us
  Pallas kernels  346 us (97%)
  local copies, waits for them, and re-layouts  5.68 us (2%)
    pallas_call x1, Pallas kernels, backward(): pl.pallas_call(functools.partial(backward_kernel, n, (rows, d, ff)), out_...  170 us
    pallas_call x1, Pallas kernels, forward(): pl.pallas_call(functools.partial(forward_kernel, n), grid=(rows // TILE,)...  98.4 us
    pallas_call x1, Pallas kernels, last(): pl.pallas_call(last_kernel, grid=(rows // TILE,), out_shape=[jax.ShapeDty...  77.6 us

profile of v2, /device:TPU:112, one launch (start us, length us, event | category | flops | bytes accessed | tf_op | source)
XLA Modules:
  0.0 355.1 jit_solution(2520093011114838838)
XLA Ops:
  0.6 98.4 %forward.1 = (bf16[4096,768]{1,0:T(8,128)(2,1)}, bf16[4096,768]{1,0:T(8,128)(2,1)}, bf16[4096,1792]{1,0:T(8,128)(2,1)}, f32[4096,1792]{1,0:T(8,128)}, f32[4096,1...) custom-call(bf16[4096,768]{1,0:T(8,128)(2,1)} %bitcast.8, ...), custom_call_target="tpu_custom_call" | custom-call | flops 33822867456 | bytes 104857600 | tf_op jit(solution)/shard_map/forward/pallas_call | solution.py:216
  99.0 77.6 %last.1 = (bf16[4096,768]{1,0:T(8,128)(2,1)}, bf16[4096,768]{1,0:T(8,128)(2,1)}, bf16[4096,1792]{1,0:T(8,128)(2,1)}, bf16[4096,1792]{1,0:T(8,128)(2,1)}, bf16[4096,1792]{1,0:T(8,128)(2,1)}) custom-call(bf16[4096,768]{1,0:T(8,128)(2,1)} %get-tuple-element.23.h_ref, bf16[4096,768]{1,0:T(8,128)(2,1)} %bitcast.6, bf16[768,1792]{1,0:T(8,128)(2,1)} %get-tuple-element.24.wg, ...), custom_call_target="tpu_custom_call" | custom-call | flops 56371445760 | bytes 83886080 | tf_op jit(solution)/shard_map/last/pallas_call | solution.py:259
  176.7 169.8 %backward.1 = (bf16[4,192,1792]{2,1,0:T(8,128)(2,1)}, bf16[2,448,768]{2,1,0:T(8,128)(2,1)}, bf16[4096,768]{1,0:T(8,128)(2,1)}, bf16[4096,1792]{1,0:T(8,128)(2,1)}, bf16[4096,1792]{1,0:T(8,128)(2,1)}) custom-call(bf16[4096,768]{1,0:T(8,128)(2,1)} %bitcast.7, bf16[4096,768]{1,0:T(8,128)(2,1)} %get-tuple-element.27.dh1, bf16[4096,768]{1,0:T(8,128)(2,1)} %bitcast.9, ...), custom_call_target="tpu_custom_call" | custom-call | flops 101468602368 | bytes 314572800 | tf_op jit(solution)/shard_map/backward/pallas_call | solution.py:637
  346.5 0.0 copy-start
  346.5 1.5 fusion.1
  348.0 0.0 slice-start
  348.0 1.2 pad_maximum_fusion.2
  349.2 0.0 copy-done
  349.2 0.0 slice-start.1
  349.2 0.2 fusion
  349.4 1.8 pad_maximum_fusion
  351.2 0.0 slice-done
  351.2 1.2 slice-done.1
  352.4 2.7 copy.10
  (1 shorter events, 0.0 us)
Async XLA Ops:
  346.5 2.8 copy-start
  348.0 3.2 slice-start
  349.2 3.2 slice-start.1

commit v3 on v2

--- a/solution.py
+++ b/solution.py
@@ -15,11 +15,24 @@
 COLS = 256
 SMALL = 256
 SLOTS = 6
-LATER = {
-    2: (("neighbours", 3), ("own", 5)),
-    3: (("neighbours", 4), ("opposite", 3)),
-    5: (("neighbours", 5), ("opposite", 4)),
-    7: (("opposite", 5),),
+LAYERS = (1, 0, 0, 0, 1, 1)
+EVENTS = {
+    0: (("greet",), ("own", 0), ("neighbours", 0), ("own", 1), ("opposite", 0), ("own", 2), ("relay", 0), ("complete", 0)),
+    1: (("neighbours", 1),),
+    2: (("own", 3),),
+    4: (("neighbours", 2),),
+    5: (("opposite", 1), ("own", 4)),
+    7: (("relay", 1),),
+    8: (("complete", 1), ("neighbours", 3)),
+    9: (("opposite", 2), ("own", 5)),
+    12: (("relay", 2),),
+    13: (("neighbours", 4),),
+    15: (("opposite", 3),),
+    16: (("relay", 3), ("complete", 2), ("complete", 3)),
+    17: (("neighbours", 5), ("opposite", 4)),
+    18: (("relay", 4), ("opposite", 5)),
+    19: (("complete", 4), ("relay", 5)),
+    20: (("complete", 5),),
 }
 
 
@@ -62,30 +75,31 @@
         self.n, self.shards, self.fulls, self.send, self.recv, self.local = n, shards, fulls, send, recv, local
         self.me = lax.axis_index("dp")
         rep = lax.axis_index("rep")
-        self.core = lax.rem(rep, 2)
-        self.partner = {"rep": rep + 1 - 2 * self.core}
+        core, chip = lax.rem(rep, 2), lax.rem(rep // 2, 2)
+        self.outer = core == chip
+        self.middle = core != chip
+        self.bring, self.given, self.far = chip + core, chip + 1 - core, 2 - 2 * chip
+        self.partner = {"rep": rep + 1 - 2 * core}
+        self.twin = {"rep": rep + 2 - 4 * chip}
         self.right = {"dp": lax.rem(self.me + 1, n)}
         self.left = {"dp": lax.rem(self.me + n - 1, n)}
 
     def shard(self, m):
-        ref = self.shards[m % 3]
-        return ref.at[m // 3]
-
-    def piece(self, m, away, quarter=None):
+        return self.shards[m % 3].at[LAYERS[m]]
+
+    def third(self, m, ref, row, which, part):
+        block, width = self.shards[m % 3].shape[1:]
+        if block % 6 == 0:
+            rows = block // 3
+            start, count = (0, rows) if part is None else (part * (rows // 2), rows // 2)
+            return ref.at[pl.ds(pl.multiple_of(row + which * rows + start, 16), count)]
+        columns = pl.ds(pl.multiple_of(which * (width // 3), 128), width // 3)
+        start, count = (0, block) if part is None else (part * (block // 2), block // 2)
+        return ref.at[pl.ds(pl.multiple_of(row + start, 16), count), columns]
+
+    def piece(self, m, which, away, part=None):
         block = self.shards[m % 3].shape[1]
-        half = block // 2
-        at = lax.rem(self.me + away + self.n, self.n) * block + self.core * half
-        if quarter is None:
-            return self.fulls[m].at[pl.ds(at, half)]
-        return self.fulls[m].at[pl.ds(at + quarter * (half // 2), half // 2)]
-
-    def other_piece(self, m, away, quarter=None):
-        block = self.shards[m % 3].shape[1]
-        half = block // 2
-        at = lax.rem(self.me + away + self.n, self.n) * block + (1 - self.core) * half
-        if quarter is None:
-            return self.fulls[m].at[pl.ds(at, half)]
-        return self.fulls[m].at[pl.ds(at + quarter * (half // 2), half // 2)]
+        return self.third(m, self.fulls[m], lax.rem(self.me + away + self.n, self.n) * block, which, part)
 
     def copy(self, m, k, src, dst, to):
         return pltpu.make_async_remote_copy(
@@ -93,23 +107,18 @@
             device_id=to, device_id_type=pl.DeviceIdType.MESH,
         )
 
-    def sends(self, m, k):
+    ARRIVALS = ((-1, None), (1, None), (2, 0), (2, 1))
+
+    def ring(self, m, k):
+        to = (self.right, self.left)[k % 2]
         if k < 2:
-            block = self.shards[m % 3].shape[1]
-            src = self.shard(m).at[pl.ds(self.core * (block // 2), block // 2)]
-            return self.copy(m, k, src, self.piece(m, 0), (self.right, self.left)[k])
-        part = {2: (-1, 0), 3: (1, 1), 4: (-1, None), 5: (1, None), 6: (2, 0), 7: (2, 1)}[k]
-        ref = self.piece(m, *part)
-        return self.copy(m, k, ref, ref, (self.right, self.left)[k - 2] if k < 4 else self.partner)
-
-    def arrives(self, m, k):
-        if k < 4:
-            part = ((-1, None), (1, None), (2, 0), (2, 1))[k]
-            ref = self.piece(m, *part)
-        else:
-            part = {4: (-1, None), 5: (1, None), 6: (2, 0), 7: (2, 1)}[k]
-            ref = self.other_piece(m, *part)
-        return self.copy(m, k, ref, ref, self.partner)
+            return self.copy(m, k, self.third(m, self.shard(m), 0, self.bring, None), self.piece(m, self.bring, 0), to)
+        ref = self.piece(m, self.bring, *((-1, 0), (1, 1))[k - 2])
+        return self.copy(m, k, ref, ref, to)
+
+    def hand(self, m, e, which, k, to):
+        ref = self.piece(m, which, *self.ARRIVALS[e])
+        return self.copy(m, k + e, ref, ref, to)
 
     def mine(self, m):
         block = self.shards[m % 3].shape[1]
@@ -117,155 +126,200 @@
 
     def greet(self):
         barrier = pltpu.get_barrier_semaphore()
-        for other in (self.left, self.right, self.partner):
+        for other in (self.left, self.right, self.partner, self.twin):
             pl.semaphore_signal(barrier, inc=1, device_id=other, device_id_type=pl.DeviceIdType.MESH)
-        pl.semaphore_wait(barrier, 3)
-
-    def start(self, m, ks):
-        for k in ks:
-            self.sends(m, k).start()
+        pl.semaphore_wait(barrier, 4)
 
     def own(self, m):
-        self.start(m, (0, 1))
+        for k in range(2):
+            self.ring(m, k).start()
         self.mine(m).start()
 
+    def arrived(self, m, e):
+        self.hand(m, e, self.bring, 0, self.partner).wait_recv()
+        if e < 2:
+            self.ring(m, 2 + e).start()
+        self.hand(m, e, self.bring, 4, self.partner).start()
+
+        @pl.when(self.outer)
+        def _():
+            self.hand(m, e, self.bring, 8, self.twin).start()
+
     def neighbours(self, m):
-        self.arrives(m, 0).wait_recv()
-        self.start(m, (2, 4))
-        self.arrives(m, 1).wait_recv()
-        self.start(m, (3, 5))
+        self.arrived(m, 0)
+        self.arrived(m, 1)
 
     def opposite(self, m):
-        self.arrives(m, 2).wait_recv()
-        self.start(m, (6,))
-        self.arrives(m, 3).wait_recv()
-        self.start(m, (7,))
+        self.arrived(m, 2)
+        self.arrived(m, 3)
+
+    def relay(self, m):
+        @pl.when(self.middle)
+        def _():
+            for e in range(4):
+                self.hand(m, e, self.far, 8, self.partner).wait_recv()
+                self.hand(m, e, self.far, 8, self.partner).start()
 
     def complete(self, m):
         self.mine(m).wait()
-        for k in range(4, 8):
-            self.arrives(m, k).wait_recv()
+        for e in range(4):
+            self.hand(m, e, self.given, 4, self.partner).wait_recv()
+
+        @pl.when(self.outer)
+        def _():
+            for e in range(4):
+                self.hand(m, e, self.far, 8, self.partner).wait_recv()
 
     def sent(self, m):
-        for k in range(8):
-            self.sends(m, k).wait_send()
-
-
-def forward_kernel(n, x, sg, su, sd, h1, a_out, act, g_out, u_out, *rest):
-    outs, fulls, (send, recv, local, out_sem) = rest[:6], rest[6:12], rest[12:]
-    gather = Gather(n, (sg, su, sd), fulls, send, recv, local)
+        for k in range(4):
+            self.ring(m, k).wait_send()
+        for e in range(4):
+            self.hand(m, e, self.bring, 4, self.partner).wait_send()
+            self.hand(m, e, self.bring, 8, self.partner).wait_send()
+
+
+def forward_kernel(n, x, dy, sd, sg, su, h1, a_out, acts, u_out, g_out, *rest):
+    outs, fulls, (g_all, send, recv, local, out_sem, g_sem) = rest[:5], rest[5:11], rest[11:]
+    gather = Gather(n, (sd, sg, su), fulls, send, recv, local)
     step = pl.program_id(0)
+    tiles = pl.num_programs(0) // 3
 
     def keep(m):
-        return pltpu.make_async_copy(fulls[m], outs[m], out_sem.at[m])
-
-    @pl.when(step == 0)
+        return pltpu.make_async_copy(fulls[m], outs[m - 1], out_sem.at[m - 1])
+
+    def complete(m):
+        gather.complete(m)
+        if m:
+            keep(m).start()
+
+    for at, events in EVENTS.items():
+        @pl.when(step == at)
+        def _():
+            for stage, *m in events:
+                (complete if stage == "complete" else getattr(gather, stage))(*m)
+
+    wd1, wg, wu, wd = fulls[:4]
+    tile, ff = x.shape[0], wg.shape[1]
+
+    def rows(t):
+        return pl.ds(pl.multiple_of(t * tile, tile), tile)
+
+    def keep_gate(t):
+        return pltpu.make_async_copy(g_all.at[rows(t)], g_out.at[rows(t)], g_sem.at[t])
+
+    @pl.when(step < tiles)
     def _():
-        gather.greet()
-        gather.own(0)
-        gather.own(1)
-        gather.neighbours(0)
-        gather.own(2)
-        gather.neighbours(1)
-        gather.opposite(0)
-        gather.own(3)
-        gather.neighbours(2)
-        gather.opposite(1)
-        gather.own(4)
-        gather.opposite(2)
-        for m in range(3):
-            gather.complete(m)
-            keep(m).start()
-
-    for at, events in LATER.items():
-        @pl.when(step == at)
-        def _():
-            for stage, m in events:
-                getattr(gather, stage)(m)
-
-    wg, wu, wd = fulls[:3]
-    h = x[...]
-    wide, scale = normed(h)
+        for s in cuts(ff, COLS):
+            acts[0, :, s] = dot_as(dy[...], wd1[s, :], NT).astype(BF16)
+
+    @pl.when((step >= tiles) & (step < 2 * tiles))
+    def _():
+        wide, scale = normed(x[...])
+        a = (wide * scale).astype(BF16)
+        a_out[...] = a
+        for s in cuts(ff, COLS):
+            g_all[rows(step - tiles), s] = dot(a, wg[:, s])
+        keep_gate(step - tiles).start()
+
+    @pl.when(step >= 2 * tiles)
+    def _():
+        h = x[...]
+        wide, scale = normed(h)
+        a = (wide * scale).astype(BF16)
+        for s in cuts(ff, COLS):
+            u = dot(a, wu[:, s])
+            g = g_all[rows(step - 2 * tiles), s]
+            u_out[:, s] = u
+            acts[0, :, s] = (g * jax.nn.sigmoid(g) * u).astype(BF16)
+        h1[...] = h + dot(acts[0], wd[...]).astype(BF16)
+
+    @pl.when(step == pl.num_programs(0) - 1)
+    def _():
+        for m in range(6):
+            gather.sent(m)
+            if m:
+                keep(m).wait()
+        for t in range(8):
+            keep_gate(t).wait()
+
+
+def forward(n, x, dy, sg, su, sd):
+    rows, d = x.shape
+    ff = sg.shape[2]
+    shapes = [(ff, d), (d, ff), (d, ff)] * 2
+    tiles = rows // TILE
+    assert tiles == 8 and n == 4
+    outs = [((rows, d), BF16), ((rows, d), BF16), ((2, rows, ff), BF16), ((rows, ff), F32), ((rows, ff), F32)] + [(s, BF16) for s in shapes[1:]]
+    anywhere = pl.BlockSpec(memory_space=pl.ANY)
+    late = lambda width: pl.BlockSpec((TILE, width), lambda i: (jnp.maximum(i - 2 * tiles, 0), 0))
+    dma = pltpu.SemaphoreType.DMA
+
+    def acts_at(i):
+        return jnp.where(i < 2 * tiles, 0, 1), jnp.where(i < 2 * tiles, jnp.minimum(i, tiles - 1), i - 2 * tiles), 0
+
+    return pl.pallas_call(
+        functools.partial(forward_kernel, n),
+        grid=(3 * tiles,),
+        out_shape=[jax.ShapeDtypeStruct(*o) for o in outs],
+        in_specs=[
+            pl.BlockSpec((TILE, d), lambda i: (lax.rem(i, tiles), 0)),
+            pl.BlockSpec((TILE, d), lambda i: (jnp.minimum(i, tiles - 1), 0)),
+        ]
+        + [anywhere] * 3,
+        out_specs=[
+            late(d),
+            pl.BlockSpec((TILE, d), lambda i: (jnp.clip(i - tiles, 0, tiles - 1), 0)),
+            pl.BlockSpec((1, TILE, ff), acts_at),
+            late(ff),
+        ]
+        + [anywhere] * 6,
+        scratch_shapes=[pltpu.VMEM(s, BF16) for s in shapes]
+        + [pltpu.VMEM((rows, ff), F32), dma((6, 12)), dma((6, 12)), dma((6,)), dma((5,)), dma((tiles,))],
+        compiler_params=pltpu.CompilerParams(
+            dimension_semantics=("arbitrary",), vmem_limit_bytes=67043328, collective_id=0, has_side_effects=True
+        ),
+        cost_estimate=cost(4, rows, d, ff, 130 * 2**20),
+        name="forward",
+    )(x, dy, sd, sg, su)
+
+
+def through_norm(wide, scale, da, dh):
+    m = jnp.mean(da * wide, -1, keepdims=True)
+    return dh + (scale * da - wide * (scale * scale * scale * m)).astype(BF16)
+
+
+def gate_grads(g, u, dact):
+    sig = jax.nn.sigmoid(g)
+    silu = g * sig
+    return silu, (dact * u * (sig + silu * (1 - sig))).astype(BF16), (dact * silu).astype(BF16)
+
+
+def last_kernel(h_ref, dy_ref, dacts, wg, wu, dh, a_out, act, dg, du):
+    wide, scale = normed(h_ref[...])
     a = (wide * scale).astype(BF16)
     a_out[...] = a
     for s in cuts(wg.shape[1], COLS):
         g = dot(a, wg[:, s])
         u = dot(a, wu[:, s])
-        g_out[:, s] = g
-        u_out[:, s] = u
-        act[:, s] = (g * jax.nn.sigmoid(g) * u).astype(BF16)
-    h1[...] = h + dot(act[...], wd[...]).astype(BF16)
-
-    @pl.when(step == pl.num_programs(0) - 1)
-    def _():
-        for m in range(3, 6):
-            gather.complete(m)
-            keep(m).start()
-        for m in range(6):
-            gather.sent(m)
-            keep(m).wait()
-
-
-def forward(n, x, sg, su, sd):
-    rows, d = x.shape
-    ff = sg.shape[2]
-    shapes = [(d, ff), (d, ff), (ff, d)] * 2
-    outs = [((rows, d), BF16), ((rows, d), BF16), ((rows, ff), BF16), ((rows, ff), F32), ((rows, ff), F32)] + [(s, BF16) for s in shapes]
-    anywhere = pl.BlockSpec(memory_space=pl.ANY)
-    assert rows // TILE == 8 and n == 4
-    return pl.pallas_call(
-        functools.partial(forward_kernel, n),
-        grid=(rows // TILE,),
-        out_shape=[jax.ShapeDtypeStruct(*o) for o in outs],
-        in_specs=[rows_of(d)] + [anywhere] * 3,
-        out_specs=[rows_of(d), rows_of(d), rows_of(ff), rows_of(ff), rows_of(ff)] + [anywhere] * 6,
-        scratch_shapes=[pltpu.VMEM(s, BF16) for s in shapes]
-        + [pltpu.SemaphoreType.DMA((6, 8)), pltpu.SemaphoreType.DMA((6, 8)), pltpu.SemaphoreType.DMA((6,)), pltpu.SemaphoreType.DMA((6,))],
-        compiler_params=params(collective_id=0, has_side_effects=True),
-        cost_estimate=cost(3, rows, d, ff, 100 * 2**20),
-        name="forward",
-    )(x, sg, su, sd)
-
-
-def through_norm(wide, scale, da, dh):
-    m = jnp.mean(da * wide, -1, keepdims=True)
-    return dh + (scale * da - wide * (scale * scale * scale * m)).astype(BF16)
-
-
-def gate_grads(g, u, dact):
-    sig = jax.nn.sigmoid(g)
-    silu = g * sig
-    return silu, (dact * u * (sig + silu * (1 - sig))).astype(BF16), (dact * silu).astype(BF16)
-
-
-def last_kernel(h_ref, dy_ref, wg, wu, wd, dh, a_out, act, dg, du):
-    wide, scale = normed(h_ref[...])
-    a = (wide * scale).astype(BF16)
-    a_out[...] = a
-    dy = dy_ref[...]
-    for s in cuts(wg.shape[1], COLS):
-        g = dot(a, wg[:, s])
-        u = dot(a, wu[:, s])
-        dact = dot_as(dy, wd[s, :], NT).astype(BF16).astype(F32)
-        silu, dg[:, s], du[:, s] = gate_grads(g, u, dact)
+        silu, dg[:, s], du[:, s] = gate_grads(g, u, dacts[0, :, s].astype(F32))
         act[:, s] = (silu * u).astype(BF16)
     da = dot_as(dg[...], wg[...], NT) + dot_as(du[...], wu[...], NT)
-    dh[...] = through_norm(wide, scale, da.astype(BF16).astype(F32), dy)
-
-
-def last(h, dy, wg, wu, wd):
+    dh[...] = through_norm(wide, scale, da.astype(BF16).astype(F32), dy_ref[...])
+
+
+def last(h, dy, acts, wg, wu):
     rows, d = h.shape
     ff = wg.shape[1]
     return pl.pallas_call(
         last_kernel,
         grid=(rows // TILE,),
         out_shape=[jax.ShapeDtypeStruct((rows, d), BF16)] * 2 + [jax.ShapeDtypeStruct((rows, ff), BF16)] * 3,
-        in_specs=[rows_of(d), rows_of(d)] + [whole(w.shape) for w in (wg, wu, wd)],
+        in_specs=[rows_of(d), rows_of(d), pl.BlockSpec((1, TILE, ff), lambda i: (0, i, 0))] + [whole(w.shape) for w in (wg, wu)],
         out_specs=[rows_of(d)] * 2 + [rows_of(ff)] * 3,
         compiler_params=params(),
-        cost_estimate=cost(5, rows, d, ff, 80 * 2**20),
+        cost_estimate=cost(4, rows, d, ff, 90 * 2**20),
         name="last",
-    )(h, dy, wg, wu, wd)
+    )(h, dy, acts, wg, wu)
 
 
 class Scatter:
@@ -325,7 +379,7 @@
 
 
 def backward_kernel(
-    n, dims, dy, dh1, x, a0, a1, act0, act1, dg1, du1, g0, u0, wg0, wu0, wd0,
+    n, dims, dy, dh1, x, a0, a1, acts, act1, dg1, du1, g0, u0, wg0, wu0, wd0,
     wide_out, down_out, dx, dg0, du0,
     ra, ract, blk, term, wd, g_t, u_t, dh_t, dg_t, du_t, x_t, dx_t,
     wk, ws1, wr1, ws2, wr2, dk, ds1, dr1, ds2, dr2,
@@ -344,7 +398,7 @@
     load_a1 = lambda: resident(a1, ra, 0)
     load_a0 = lambda: resident(a0, ra, 0)
     load_act1 = lambda: resident(act1, ract, 1)
-    load_act0 = lambda: resident(act0, ract, 1)
+    load_act0 = lambda: resident(acts.at[1], ract, 1)
     load_wd = lambda: resident(wd0, wd, 2)
     load_wg = lambda: resident(wg0, ract.at[pl.ds(0, d)], 1)
     load_wu = lambda: resident(wu0, ract.at[pl.ds(d, d)], 2)
@@ -616,7 +670,7 @@
         late_out(t).wait()
 
 
-def backward(n, dy, dh1, x, a0, a1, act0, act1, dg1, du1, g0, u0, wg0, wu0, wd0):
+def backward(n, dy, dh1, x, a0, a1, acts, act1, dg1, du1, g0, u0, wg0, wu0, wd0):
     rows, d = dy.shape
     ff = act1.shape[1]
     wide, down = d // n, ff // n
@@ -666,7 +720,7 @@
         compiler_params=pltpu.CompilerParams(vmem_limit_bytes=67043328, collective_id=1, has_side_effects=True),
         cost_estimate=cost(9, rows, d, ff, 300 * 2**20),
         name="backward",
-    )(dy, dh1, x, a0, a1, act0, act1, dg1, du1, g0, u0, wg0, wu0, wd0)
+    )(dy, dh1, x, a0, a1, acts, act1, dg1, du1, g0, u0, wg0, wu0, wd0)
 
 
 def solution(mesh):
@@ -674,9 +728,9 @@
 
     def body(x, dy, sg, su, sd):
         x, dy = x[0], dy[0]
-        h1, a0, act0, g0, u0, wg0, wu0, wd0, wg1, wu1, wd1 = forward(n, x, sg, su, sd)
-        dh1, a1, act1, dg1, du1 = last(h1, dy, wg1, wu1, wd1)
-        wide, down, dx, _, _ = backward(n, dy, dh1, x, a0, a1, act0, act1, dg1, du1, g0, u0, wg0, wu0, wd0)
+        h1, a0, acts, u0, g0, wg0, wu0, wd0, wg1, wu1 = forward(n, x, dy, sg, su, sd)
+        dh1, a1, act1, dg1, du1 = last(h1, dy, acts, wg1, wu1)
+        wide, down, dx, _, _ = backward(n, dy, dh1, x, a0, a1, acts, act1, dg1, du1, g0, u0, wg0, wu0, wd0)
         gate1, up1, gate0, up0 = wide
         down1, down0 = down
         return dx[None], jnp.stack([gate0, gate1]), jnp.stack([up0, up1]), jnp.stack([down0, down1])

time: 355 us -> 338 us (0.952); the launches traced: 355 us -> 334 us
  Pallas kernels: 346 us -> 325 us
    pallas_call x1, Pallas kernels: 77.6 us -> 58.9 us  [last(): pl.pallas_call(last_kernel, grid=(rows // TILE,), out_shape=[jax.ShapeDty...]
    pallas_call x1, Pallas kernels: 170 us -> 165 us  [backward(): pl.pallas_call(functools.partial(backward_kernel, n, (rows, d, ff)), out_...]
where the time goes in v3:
time: 338 us; the launch traced here: 334 us
  Pallas kernels  325 us (96%)
  local copies, waits for them, and re-layouts  5.68 us (2%)
    pallas_call x1, Pallas kernels, backward(): pl.pallas_call(functools.partial(backward_kernel, n, (rows, d, ff)), out_...  165 us
    pallas_call x1, Pallas kernels, forward(): pl.pallas_call(functools.partial(forward_kernel, n), grid=(3 * tiles,), o...  101 us
    pallas_call x1, Pallas kernels, last(): pl.pallas_call(last_kernel, grid=(rows // TILE,), out_shape=[jax.ShapeDty...  58.9 us

profile of v3, /device:TPU:112, one launch (start us, length us, event | category | flops | bytes accessed | tf_op | source)
XLA Modules:
  0.0 334.2 jit_solution(17156749411635544025)
XLA Ops:
  0.6 100.7 %forward.1 = (bf16[4096,768]{1,0:T(8,128)(2,1)}, bf16[4096,768]{1,0:T(8,128)(2,1)}, bf16[2,4096,1792]{2,1,0:T(8,128)(2,1)}, f32[4096,1792]{1,0:T(8,128)}, f32[40...) custom-call(bf16[4096,768]{1,0:T(8,128)(2,1)} %bitcast.9, ...), custom_call_target="tpu_custom_call" | custom-call | flops 45097156608 | bytes 136314880 | tf_op jit(solution)/shard_map/forward/pallas_call | solution.py:260
  101.4 58.9 %last.1 = (bf16[4096,768]{1,0:T(8,128)(2,1)}, bf16[4096,768]{1,0:T(8,128)(2,1)}, bf16[4096,1792]{1,0:T(8,128)(2,1)}, bf16[4096,1792]{1,0:T(8,128)(2,1)}, bf16[4096,1792]{1,0:T(8,128)(2,1)}) custom-call(bf16[4096,768]{1,0:T(8,128)(2,1)} %get-tuple-element.22.h_ref, bf16[4096,768]{1,0:T(8,128)(2,1)} %bitcast.7, ...), custom_call_target="tpu_custom_call" | custom-call | flops 45097156608 | bytes 94371840 | tf_op jit(solution)/shard_map/last/pallas_call | solution.py:313
  160.2 165.2 %backward.1 = (bf16[4,192,1792]{2,1,0:T(8,128)(2,1)}, bf16[2,448,768]{2,1,0:T(8,128)(2,1)}, bf16[4096,768]{1,0:T(8,128)(2,1)}, bf16[4096,1792]{1,0:T(8,128)(2,1)}, bf16[4096,1792]{1,0:T(8,128)(2,1)}) custom-call(bf16[4096,768]{1,0:T(8,128)(2,1)} %bitcast.8, bf16[4096,768]{1,0:T(8,128)(2,1)} %get-tuple-element.26.dh1, bf16[4096,768]{1,0:T(8,128)(2,1)} %bitcast.10, ...), custom_call_target="tpu_custom_call" | custom-call | flops 101468602368 | bytes 314572800 | tf_op jit(solution)/shard_map/backward/pallas_call | solution.py:691
  325.5 0.0 copy-start
  325.5 1.5 fusion.1
  327.0 0.0 slice-start
  327.0 1.2 pad_maximum_fusion.2
  328.2 0.0 copy-done
  328.3 0.0 slice-start.1
  328.3 0.2 fusion
  328.4 1.8 pad_maximum_fusion
  330.2 0.0 slice-done
  330.2 1.2 slice-done.1
  331.5 2.7 copy.10
  (1 shorter events, 0.0 us)
Async XLA Ops:
  325.5 2.8 copy-start
  327.0 3.2 slice-start
  328.3 3.2 slice-start.1

commit v4 on v3

--- a/solution.py
+++ b/solution.py
@@ -14,24 +14,26 @@
 TILE = 512
 COLS = 256
 SMALL = 256
-SLOTS = 6
+SLOTS = 9
+ON, DONE = 4, 8
 LAYERS = (1, 0, 0, 0, 1, 1)
 EVENTS = {
-    0: (("greet",), ("own", 0), ("neighbours", 0), ("own", 1), ("opposite", 0), ("own", 2), ("relay", 0), ("complete", 0)),
-    1: (("neighbours", 1),),
-    2: (("own", 3),),
-    4: (("neighbours", 2),),
-    5: (("opposite", 1), ("own", 4)),
-    7: (("relay", 1),),
-    8: (("complete", 1), ("neighbours", 3)),
-    9: (("opposite", 2), ("own", 5)),
-    12: (("relay", 2),),
-    13: (("neighbours", 4),),
-    15: (("opposite", 3),),
-    16: (("relay", 3), ("complete", 2), ("complete", 3)),
-    17: (("neighbours", 5), ("opposite", 4)),
-    18: (("relay", 4), ("opposite", 5)),
-    19: (("complete", 4), ("relay", 5)),
+    0: (
+        ("greet",), ("own", 0), ("neighbours", 0), ("own", 1), ("opposite", 0), ("own", 2), ("relay", 0), ("neighbours", 1), ("own", 3), ("complete", 0),
+    ),
+    3: (("opposite", 1), ("neighbours", 2), ("own", 4)),
+    5: (("relay", 1),),
+    6: (("opposite", 2), ("neighbours", 3), ("own", 5)),
+    8: (("complete", 1),),
+    9: (("relay", 2),),
+    10: (("opposite", 3),),
+    12: (("neighbours", 4),),
+    13: (("relay", 3),),
+    14: (("opposite", 4), ("neighbours", 5)),
+    16: (("complete", 2), ("complete", 3)),
+    17: (("relay", 4), ("opposite", 5)),
+    18: (("complete", 4),),
+    19: (("relay", 5),),
     20: (("complete", 5),),
 }
 
@@ -388,7 +390,7 @@
     rows, d, ff = dims
     tiles = rows // SMALL
     wides, downs = ff // COLS, d // COLS
-    first_tiles = tiles // 2 - downs
+    first_tiles = tiles // 2 - downs + 1
     wide = Scatter(n, d // n, wk, ws1, wr1, ws2, wr2, wsend, wrecv)
     down = Scatter(n, ff // n, dk, ds1, dr1, ds2, dr2, dsend, drecv)
 
@@ -431,8 +433,8 @@
         return ref.at[pl.ds(pl.multiple_of(t * SMALL, SMALL), SMALL)]
 
     def tile_in(t):
-        slot = lax.rem(t, 2)
-        return [pltpu.make_async_copy(tile_of(src, t), dst.at[slot], in_sem.at[k, slot]) for k, (src, dst) in enumerate(((g0, g_t), (u0, u_t), (dh1, dh_t)))]
+        pairs = ((g0, g_t), (u0, u_t), (dh1, dh_t.at[0]))
+        return [pltpu.make_async_copy(tile_of(src, t), dst, in_sem.at[k, 0]) for k, (src, dst) in enumerate(pairs)]
 
     def tile_out(t):
         slot = lax.rem(t, 2)
@@ -443,20 +445,21 @@
         for c in tile_in(t):
             c.wait()
 
+        @pl.when(t >= 2)
+        def _():
+            for c in tile_out(t - 2):
+                c.wait()
+
+        dh = dh_t[0]
+        for s in cuts(ff, COLS):
+            dact = dot_as(dh, wd[s, :], NT).astype(BF16).astype(F32)
+            _, dg_t[slot, :, s], du_t[slot, :, s] = gate_grads(g_t[:, s], u_t[:, s], dact)
+
         @pl.when(t + 1 < tiles)
         def _():
             for c in tile_in(t + 1):
                 c.start()
 
-        @pl.when(t >= 2)
-        def _():
-            for c in tile_out(t - 2):
-                c.wait()
-
-        dh = dh_t[slot]
-        for s in cuts(ff, COLS):
-            dact = dot_as(dh, wd[s, :], NT).astype(BF16).astype(F32)
-            _, dg_t[slot, :, s], du_t[slot, :, s] = gate_grads(g_t[slot, :, s], u_t[slot, :, s], dact)
         for c in tile_out(t):
             c.start()
 
@@ -494,61 +497,63 @@
     def end_down(r, j):
         down_out[r, :, pl.ds(pl.multiple_of(j * COLS, COLS), COLS)] = down.end(j)
 
+    def send_wide(k):
+        wide.middle(lax.rem(k, SLOTS))
+
+    def send_down(r, j):
+        down.middle(j)
+
     def due_wide(r, i):
         k = wides * r + i
-
-        @pl.when(i >= 2)
-        def _():
-            wide.middle(lax.rem(k + SLOTS - 2, SLOTS))
-
-        @pl.when((r >= 1) & (i < 2))
-        def _():
-            down.middle(i + downs - 2)
-
-        @pl.when(i >= 4)
-        def _():
-            end_wide(k - 4)
-
-        @pl.when((r >= 1) & (i == 0))
-        def _():
-            end_wide(k - 1)
-
-        @pl.when((r >= 1) & (i >= 1) & (i < 4))
-        def _():
-            end_down(r - 1, i - 1)
+        for lag, on_wide, on_down in ((ON, send_wide, send_down), (DONE, end_wide, end_down)):
+            @pl.when(i >= lag)
+            def _():
+                on_wide(k - lag)
+
+            @pl.when((r >= 1) & (i >= lag - downs) & (i < lag))
+            def _():
+                on_down(r - 1, i + downs - lag)
+
+            if lag > downs:
+                @pl.when((r >= 1) & (i < lag - downs))
+                def _():
+                    on_wide(k + downs - lag)
 
     def due_down(r, j):
-        k = wides * r + wides + j
-
-        @pl.when(j < 2)
-        def _():
-            wide.middle(lax.rem(k - 2, SLOTS))
-
-        @pl.when(j == 2)
-        def _():
-            down.middle(0)
-
-        end_wide(k - 4)
+        for lag, on_wide, on_down in ((ON, send_wide, send_down), (DONE, end_wide, end_down)):
+            if lag < downs:
+                @pl.when(j >= lag)
+                def _():
+                    on_down(r, j - lag)
+
+            @pl.when((j < lag) & (wides + j >= lag))
+            def _():
+                on_wide(wides * r + wides + j - lag)
+
+            if lag > wides:
+                @pl.when((r >= 1) & (wides + j < lag))
+                def _():
+                    on_down(r - 1, downs + wides + j - lag)
 
     def wide_step(r, i, slot, tail):
         term[0:d, :] = dot_as(ra[...], blk[slot], TN)
         k = lax.rem(wides * r + i, SLOTS)
         wide.put(k, term)
         due_wide(r, i)
+        wide.begin(k)
         tail()
-        wide.begin(k)
 
     load_a1().start()
     load_wide(0, 0, 0)
     load_wd().start()
-    for c in tile_in(0):
-        c.start()
-    load_act1().start()
     barrier = pltpu.get_barrier_semaphore()
     for other in (wide.left, wide.right):
         pl.semaphore_signal(barrier, inc=1, device_id=other, device_id_type=pl.DeviceIdType.MESH)
     pl.semaphore_wait(barrier, 2)
     load_a1().wait()
+    for c in tile_in(0):
+        c.start()
+    load_act1().start()
     load_wd().wait()
 
     def round_(r, _):
@@ -596,12 +601,23 @@
             def _():
                 load_wide(r + 1, 0, 1 - slot)
 
+            @pl.when((j + 1 == downs) & (r == 1))
+            def _():
+                for t in (tiles - 2, tiles - 1):
+                    for c in tile_out(t):
+                        c.wait()
+                column(dg0, 0, 1 - slot).start()
+
             for s in cuts(ff, ff // 2):
                 term[s, :] = dot_as(ract[:, s], blk[slot], TN)
             down.put(j, term)
             due_down(r, j)
-            tile(r * (tiles // 2) + first_tiles + j)
             down.begin(j)
+
+            @pl.when(j + 1 < downs)
+            def _():
+                tile(r * (tiles // 2) + first_tiles + j)
+
             return 0
 
         lax.fori_loop(0, downs, down_block, 0)
@@ -614,18 +630,12 @@
 
     lax.fori_loop(0, 2, round_, 0)
 
-    for t in (tiles - 2, tiles - 1):
-        for c in tile_out(t):
-            c.wait()
     last_q = 2 * (wides + downs)
-    load_last(0, last_q % 2)
     load_wg().start()
     load_wu().start()
     for c in late_in(0):
         c.start()
     load_a0().wait()
-    load_wg().wait()
-    load_wu().wait()
     blocks = 2 * wides
     late_early = tiles // 2
 
@@ -642,6 +652,11 @@
 
             @pl.when(((i + 1) * late_early) // blocks > at)
             def _():
+                @pl.when(at == 0)
+                def _():
+                    load_wg().wait()
+                    load_wu().wait()
+
                 late(at)
 
         wide_step(2, i, slot, tail)
@@ -652,20 +667,20 @@
     def rest(v, _):
         k = 2 * wides + blocks + v
 
-        def pair(p, _):
-            late(late_early + 2 * v + p)
+        def one(t, _):
+            late(late_early + t)
             return 0
 
-        lax.fori_loop(0, 2, pair, 0)
-
-        @pl.when(v < 2)
-        def _():
-            wide.middle(lax.rem(k - 2, SLOTS))
-
-        end_wide(k - 4)
+        lax.fori_loop((v * late_early) // DONE, ((v + 1) * late_early) // DONE, one, 0)
+
+        @pl.when(v < ON)
+        def _():
+            send_wide(k - ON)
+
+        end_wide(k - DONE)
         return 0
 
-    lax.fori_loop(0, 4, rest, 0)
+    lax.fori_loop(0, DONE, rest, 0)
     for t in (tiles - 2, tiles - 1):
         late_out(t).wait()
 
@@ -705,8 +720,8 @@
             pltpu.VMEM((2, rows, COLS), BF16),
             pltpu.VMEM((ff, COLS), F32),
             pltpu.VMEM((ff, d), BF16),
-            pltpu.VMEM((2, SMALL, ff), F32),
-            pltpu.VMEM((2, SMALL, ff), F32),
+            pltpu.VMEM((SMALL, ff), F32),
+            pltpu.VMEM((SMALL, ff), F32),
             pltpu.VMEM((2, SMALL, d), BF16),
             pltpu.VMEM((2, SMALL, ff), BF16),
             pltpu.VMEM((2, SMALL, ff), BF16),

time: 338 us -> 324 us (0.959); the launches traced: 334 us -> 324 us
  Pallas kernels: 325 us -> 315 us
    pallas_call x1, Pallas kernels: 101 us -> 92.7 us  [forward(): pl.pallas_call(functools.partial(forward_kernel, n), grid=(3 * tiles,), o...]
where the time goes in v4:
time: 324 us
  Pallas kernels  315 us (97%)
  local copies, waits for them, and re-layouts  5.68 us (2%)
    pallas_call x1, Pallas kernels, backward(): pl.pallas_call(functools.partial(backward_kernel, n, (rows, d, ff)), out_...  163 us
    pallas_call x1, Pallas kernels, forward(): pl.pallas_call(functools.partial(forward_kernel, n), grid=(3 * tiles,), o...  92.7 us
    pallas_call x1, Pallas kernels, last(): pl.pallas_call(last_kernel, grid=(rows // TILE,), out_shape=[jax.ShapeDty...  58.9 us

profile of v4, /device:TPU:112, one launch (start us, length us, event | category | flops | bytes accessed | tf_op | source)
XLA Modules:
  0.0 324.2 jit_solution(3392907768780935047)
XLA Ops:
  0.6 92.7 %forward.1 = (bf16[4096,768]{1,0:T(8,128)(2,1)}, bf16[4096,768]{1,0:T(8,128)(2,1)}, bf16[2,4096,1792]{2,1,0:T(8,128)(2,1)}, f32[4096,1792]{1,0:T(8,128)}, f32[40...) custom-call(bf16[4096,768]{1,0:T(8,128)(2,1)} %bitcast.9, ...), custom_call_target="tpu_custom_call" | custom-call | flops 45097156608 | bytes 136314880 | tf_op jit(solution)/shard_map/forward/pallas_call | solution.py:262
  93.3 58.9 %last.1 = (bf16[4096,768]{1,0:T(8,128)(2,1)}, bf16[4096,768]{1,0:T(8,128)(2,1)}, bf16[4096,1792]{1,0:T(8,128)(2,1)}, bf16[4096,1792]{1,0:T(8,128)(2,1)}, bf16[4096,1792]{1,0:T(8,128)(2,1)}) custom-call(bf16[4096,768]{1,0:T(8,128)(2,1)} %get-tuple-element.22.h_ref, bf16[4096,768]{1,0:T(8,128)(2,1)} %bitcast.7, ...), custom_call_target="tpu_custom_call" | custom-call | flops 45097156608 | bytes 94371840 | tf_op jit(solution)/shard_map/last/pallas_call | solution.py:315
  152.2 163.3 %backward.1 = (bf16[4,192,1792]{2,1,0:T(8,128)(2,1)}, bf16[2,448,768]{2,1,0:T(8,128)(2,1)}, bf16[4096,768]{1,0:T(8,128)(2,1)}, bf16[4096,1792]{1,0:T(8,128)(2,1)}, bf16[4096,1792]{1,0:T(8,128)(2,1)}) custom-call(bf16[4096,768]{1,0:T(8,128)(2,1)} %bitcast.8, bf16[4096,768]{1,0:T(8,128)(2,1)} %get-tuple-element.26.dh1, bf16[4096,768]{1,0:T(8,128)(2,1)} %bitcast.10, ...), custom_call_target="tpu_custom_call" | custom-call | flops 101468602368 | bytes 314572800 | tf_op jit(solution)/shard_map/backward/pallas_call | solution.py:706
  315.5 0.0 copy-start
  315.5 1.5 fusion.1
  317.1 0.0 slice-start
  317.1 1.2 pad_maximum_fusion.2
  318.3 0.0 copy-done
  318.3 0.0 slice-start.1
  318.3 0.2 fusion
  318.5 1.8 pad_maximum_fusion
  320.3 0.0 slice-done
  320.3 1.2 slice-done.1
  321.5 2.7 copy.10
  (1 shorter events, 0.0 us)
Async XLA Ops:
  315.5 2.8 copy-start
  317.1 3.2 slice-start
  318.3 3.2 slice-start.1

commit v5 on v4

--- a/solution.py
+++ b/solution.py
@@ -18,20 +18,18 @@
 ON, DONE = 4, 8
 LAYERS = (1, 0, 0, 0, 1, 1)
 EVENTS = {
-    0: (
-        ("greet",), ("own", 0), ("neighbours", 0), ("own", 1), ("opposite", 0), ("own", 2), ("relay", 0), ("neighbours", 1), ("own", 3), ("complete", 0),
-    ),
-    3: (("opposite", 1), ("neighbours", 2), ("own", 4)),
-    5: (("relay", 1),),
-    6: (("opposite", 2), ("neighbours", 3), ("own", 5)),
+    0: (("greet",), ("own", 0), ("neighbours", 0), ("own", 1), ("opposite", 0), ("own", 2), ("relay", 0), ("neighbours", 1), ("own", 3), ("complete", 0),),
+    4: (("opposite", 1), ("neighbours", 2), ("own", 4),),
+    6: (("relay", 1),),
+    7: (("opposite", 2), ("neighbours", 3), ("own", 5),),
     8: (("complete", 1),),
-    9: (("relay", 2),),
-    10: (("opposite", 3),),
-    12: (("neighbours", 4),),
-    13: (("relay", 3),),
-    14: (("opposite", 4), ("neighbours", 5)),
-    16: (("complete", 2), ("complete", 3)),
-    17: (("relay", 4), ("opposite", 5)),
+    10: (("relay", 2),),
+    11: (("opposite", 3),),
+    13: (("neighbours", 4),),
+    14: (("relay", 3),),
+    15: (("opposite", 4), ("neighbours", 5),),
+    16: (("complete", 2), ("complete", 3),),
+    17: (("relay", 4), ("opposite", 5),),
     18: (("complete", 4),),
     19: (("relay", 5),),
     20: (("complete", 5),),

time: 324 us -> 323 us (level)
  no operation moved by 1% of the time
where the time goes in v5:
time: 323 us
  Pallas kernels  314 us (97%)
  local copies, waits for them, and re-layouts  5.68 us (2%)
    pallas_call x1, Pallas kernels, backward(): pl.pallas_call(functools.partial(backward_kernel, n, (rows, d, ff)), out_...  164 us
    pallas_call x1, Pallas kernels, forward(): pl.pallas_call(functools.partial(forward_kernel, n), grid=(3 * tiles,), o...  91.4 us
    pallas_call x1, Pallas kernels, last(): pl.pallas_call(last_kernel, grid=(rows // TILE,), out_shape=[jax.ShapeDty...  58.9 us

profile of v5, /device:TPU:112, one launch (start us, length us, event | category | flops | bytes accessed | tf_op | source)
XLA Modules:
  0.0 323.3 jit_solution(7733431599272983327)
XLA Ops:
  0.6 91.4 %forward.1 = (bf16[4096,768]{1,0:T(8,128)(2,1)}, bf16[4096,768]{1,0:T(8,128)(2,1)}, bf16[2,4096,1792]{2,1,0:T(8,128)(2,1)}, f32[4096,1792]{1,0:T(8,128)}, f32[40...) custom-call(bf16[4096,768]{1,0:T(8,128)(2,1)} %bitcast.9, ...), custom_call_target="tpu_custom_call" | custom-call | flops 45097156608 | bytes 136314880 | tf_op jit(solution)/shard_map/forward/pallas_call | solution.py:260
  92.0 58.9 %last.1 = (bf16[4096,768]{1,0:T(8,128)(2,1)}, bf16[4096,768]{1,0:T(8,128)(2,1)}, bf16[4096,1792]{1,0:T(8,128)(2,1)}, bf16[4096,1792]{1,0:T(8,128)(2,1)}, bf16[4096,1792]{1,0:T(8,128)(2,1)}) custom-call(bf16[4096,768]{1,0:T(8,128)(2,1)} %get-tuple-element.22.h_ref, bf16[4096,768]{1,0:T(8,128)(2,1)} %bitcast.7, ...), custom_call_target="tpu_custom_call" | custom-call | flops 45097156608 | bytes 94371840 | tf_op jit(solution)/shard_map/last/pallas_call | solution.py:313
  150.9 163.7 %backward.1 = (bf16[4,192,1792]{2,1,0:T(8,128)(2,1)}, bf16[2,448,768]{2,1,0:T(8,128)(2,1)}, bf16[4096,768]{1,0:T(8,128)(2,1)}, bf16[4096,1792]{1,0:T(8,128)(2,1)}, bf16[4096,1792]{1,0:T(8,128)(2,1)}) custom-call(bf16[4096,768]{1,0:T(8,128)(2,1)} %bitcast.8, bf16[4096,768]{1,0:T(8,128)(2,1)} %get-tuple-element.26.dh1, bf16[4096,768]{1,0:T(8,128)(2,1)} %bitcast.10, ...), custom_call_target="tpu_custom_call" | custom-call | flops 101468602368 | bytes 314572800 | tf_op jit(solution)/shard_map/backward/pallas_call | solution.py:704
  314.6 0.0 copy-start
  314.6 1.5 fusion.1
  316.1 0.0 slice-start
  316.2 1.2 pad_maximum_fusion.2
  317.3 0.0 copy-done
  317.4 0.0 slice-start.1
  317.4 0.2 fusion
  317.5 1.8 pad_maximum_fusion
  319.3 0.0 slice-done
  319.3 1.2 slice-done.1
  320.6 2.7 copy.10
  (1 shorter events, 0.0 us)
Async XLA Ops:
  314.6 2.8 copy-start
  316.1 3.2 slice-start
  317.4 3.2 slice-start.1
